TPU v7x, 16 devices: a whole 2x2x2 slice. The times are simulated.
16 devices in a mesh: dp: 1, tp: 16 (over x, y, z, core).
Axes of the slice: x: 2, y: 2, z: 2, core: 2. Of those that a mesh axis runs over, the one named last changes fastest.
Arguments:
- x: bfloat16 [2048, 12288], P('dp')
- w_gate: bfloat16 [12288, 28672], P(None, 'tp')
- w_up: bfloat16 [12288, 28672], P(None, 'tp')
- w_down: bfloat16 [28672, 12288], P('tp')
Outputs:
- output: bfloat16 [2048, 12288], P('dp')
All inputs are finite; a program needn't handle non-finite values.
Results may differ from a plain program's by a relative error of at most 0.016.
Values are sent between devices in bfloat16 or wider.
A program may use at most 2 GiB of HBM per device.

v0:
```python
import jax
import jax.numpy as jnp
from jax import lax
from jax.sharding import PartitionSpec as P


def solution(mesh):
    def step(x, w_gate, w_up, w_down):
        gate = jnp.dot(x, w_gate, preferred_element_type=jnp.float32)
        up = jnp.dot(x, w_up, preferred_element_type=jnp.float32)
        hidden = (jax.nn.silu(gate) * up).astype(jnp.bfloat16)
        term = jnp.dot(hidden, w_down, preferred_element_type=jnp.float32).astype(jnp.bfloat16)
        return lax.psum(term, "tp")

    return jax.shard_map(
        step,
        mesh=mesh,
        in_specs=(P("dp", None), P(None, "tp"), P(None, "tp"), P("tp", None)),
        out_specs=P("dp", None),
        check_vma=False,
    )
```

profile of v0, /device:TPU:0, one launch (start us, length us, event | category | flops | bytes accessed | tf_op | source)
XLA Modules:
  0.0 809.8 jit_solution(162394332292201179)
XLA Ops:
  6.5 0.0 all-reduce.2.cloned.1.call-start
  6.5 101.5 %fusion = f32[2048,1792]{1,0:T(8,128)} fusion(bf16[2048,12288]{1,0:T(8,128)(2,1)} %param.4, bf16[12288,1792]{1,0:T(8,128)(2,1)} %param.5), kind=kOutput, calls=%fused_computation.2 | convolution fusion | flops 90194313216 | bytes 109051904 | tf_op jit(solution)/shard_map/dot_general | solution.py:9
  108.1 105.4 %multiply_convert_fusion = bf16[2048,1792]{1,0:T(8,128)(2,1)} fusion(f32[2048,1792]{1,0:T(8,128)} %fusion, bf16[2048,12288]{1,0:T(8,128)(2,1)} %param.4, bf16[12288,1792]{1,0:T(8,128)(2,1)} %param.6), kind=kOutput, calls=%fused_computation.1 | convolution fusion | flops 90216333312 | bytes 116391936 | tf_op jit(solution)/shard_map/dot_general | solution.py:10
  213.5 100.0 %convolution_convert_fusion = bf16[2048,12288]{1,0:T(8,128)(2,1)} fusion(bf16[2048,1792]{1,0:T(8,128)(2,1)} %multiply_convert_fusion, bf16[1792,12288]{1,0:T(8,128)(2,1)} %param.7), kind=kOutput, calls=%fused_computation | convolution fusion | flops 90219479040 | bytes 101711872 | tf_op jit(solution)/shard_map/dot_general | solution.py:12
  313.4 0.0 all-reduce.2.cloned.1.call-update
  313.5 455.8 %all-reduce.2.cloned.1.call-done = bf16[2048,12288]{1,0:T(8,128)(2,1)} async-done(((bf16[2048,12288]{1,0:T(8,128)(2,1)}), bf16[2048,12288]{1,0:T(8,128)(2,1)}) %all-reduce.2.cloned.1.call-update) | async-done | bytes 50331664 | tf_op jit(solution)/shard_map/psum | solution.py:13
  769.2 33.7 %copy.6 = bf16[2048,12288]{1,0:T(8,128)(2,1)} copy(bf16[2048,12288]{1,0:T(8,128)(2,1)} %all-reduce.2.cloned.1.call-done) | data formatting | bytes 100663296
Async XLA Ops:
  6.5 762.7 %all-reduce.2.cloned.1.call-start = ((), (), s32[]{:S(2)}) async-start(), calls=%async_computation | async-start | bytes 100663296 | tf_op jit(solution)/shard_map/psum | solution.py:13
Sparse Core Ops, SparseCore 0:
  313.6 455.5 all-reduce.1
where the time goes:
time: 810 us
  waiting for transfers between devices  456 us (56%)
  matrix products  307 us (38%)
  local copies, waits for them, and re-layouts  33.7 us (4%)
  between operations  13.4 us (2%)
    psum x1, waiting for transfers between devices, step(): return lax.psum(term, 'tp')  456 us
    dot_general x1, matrix products, step(): up = jnp.dot(x, w_up, preferred_element_type=jnp.float32)  105 us
    dot_general x1, matrix products, step(): gate = jnp.dot(x, w_gate, preferred_element_type=jnp.float32)  102 us
    dot_general x1, matrix products, step(): jnp.dot(hidden, w_down, preferred_element_type=jnp.float32)  100 us
    unnamed x1, local copies, waits for them, and re-layouts  33.7 us
  transfers between devices with their start and end apart: 1, of which 1 were waited for; matrix products, arithmetic and copies ran while one was open for 0% of the time, Pallas kernels for 0%

commit v1 on v0

v1 whole, which is shorter than its diff:
```python
import functools

import jax
import jax.numpy as jnp
from jax import lax
from jax.experimental import pallas as pl
from jax.experimental.pallas import tpu as pltpu
from jax.sharding import PartitionSpec as P

MESH = pl.DeviceIdType.MESH
F32, BF16 = jnp.float32, jnp.bfloat16

R = 512
HALF = R // 2
CB = 512
KB = 6144
GN = 256
WD_STEPS = 27


def kernel(x_hbm, wg_hbm, wu_hbm, wd_hbm, y_hbm,
           xv, wbuf, acc, hv, dbuf, rv0, rv1, rv2, rv3, st0, st1, st2, st3, stf,
           x_sem, w_sem, d_sem, s0s, s1s, s2s, s3s, fs, fl, a3s, a2s, a1s,
           r0, r1, r2, r3, g3, g2, g1, g0, credit):
    rows, depth = x_hbm.shape
    units = wg_hbm.shape[1]
    nc = rows // R
    nt = units // GN
    me = lax.axis_index("tp")
    b0 = lax.rem(me, 2)

    def dim(k, s):
        return lax.rem(k + s, 3)

    def mask(d):
        return jnp.where(d == 0, 8, jnp.where(d == 1, 4, 2))

    def bit(d):
        return lax.rem(me // mask(d), 2)

    def peer(d):
        m = mask(d)
        return me + m - 2 * m * bit(d)

    core_peer = me + 1 - 2 * b0

    def bits(k):
        return bit(dim(k, 0)), bit(dim(k, 1)), bit(dim(k, 2))

    def col(k, i0, i1, i2):
        return pl.multiple_of((k * 8 + i0 * 4 + i1 * 2 + i2) * CB, CB)

    def to(dev):
        return dict(device_id={"tp": dev}, device_id_type=MESH)

    barrier = pltpu.get_barrier_semaphore()
    everyone = [peer(0), peer(1), peer(2), core_peer]
    for dev in everyone:
        pl.semaphore_signal(barrier, inc=1, **to(dev))
    pl.semaphore_wait(barrier, 4)

    def w_copies(q):
        n, kk, slot = lax.rem(q // 2, nt), lax.rem(q, 2), lax.rem(q, 2)
        src = (pl.ds(pl.multiple_of(kk * KB, KB), KB), pl.ds(pl.multiple_of(n * GN, GN), GN))
        return [
            pltpu.make_async_copy(wg_hbm.at[src], wbuf.at[slot, :, pl.ds(0, GN)], w_sem.at[slot, 0]),
            pltpu.make_async_copy(wu_hbm.at[src], wbuf.at[slot, :, pl.ds(GN, GN)], w_sem.at[slot, 1]),
        ]

    def w_start(q):
        @pl.when(q < nc * nt * 2)
        def _():
            for c in w_copies(q):
                c.start()

    def wd_col(step):
        r = lax.rem(step, WD_STEPS)
        early = r < 18
        group = r // 6
        k = jnp.where(early, lax.rem(r, 6) // 2, lax.rem(r, 3))
        j = lax.rem(r, 2)
        s1, s2, _ = bits(k)
        i0 = jnp.where(early & (group != 1), 1 - b0, b0)
        i1 = jnp.where(early & (group != 2), 1 - s1, s1)
        flip = (early & (j == 0)) | (r // 3 == 6)
        i2 = jnp.where(flip, 1 - s2, s2)
        return col(k, i0, i1, i2)

    def d_copy(step):
        slot = lax.rem(step, 3)
        return pltpu.make_async_copy(wd_hbm.at[:, pl.ds(wd_col(step), CB)], dbuf.at[slot], d_sem.at[slot])

    def d_start(step):
        @pl.when(step < nc * WD_STEPS)
        def _():
            d_copy(step).start()

    def d_next(step):
        d_copy(step).wait()
        d_start(step + 2)
        return lax.rem(step, 3)

    def x_copies(c):
        return [
            pltpu.make_async_copy(
                x_hbm.at[pl.ds(pl.multiple_of(c * R, R), R), pl.ds(i * KB, KB)], xv.at[i], x_sem.at[i]
            )
            for i in range(2)
        ]

    for c in x_copies(0):
        c.start()
    w_start(0)
    w_start(1)
    d_start(0)
    d_start(1)

    def gate_up(c, n):
        q = (c * nt + n) * 2
        for kk in range(2):
            for cp in w_copies(q + kk):
                cp.wait()
            d = jnp.dot(xv[kk], wbuf[kk], preferred_element_type=F32)
            if kk == 0:
                acc[...] = d
            else:
                t = acc[...] + d
                h = jax.nn.silu(t[:, :GN]) * t[:, GN:]
                hv[lax.rem(c, 2), :, pl.ds(pl.multiple_of(n * GN, GN), GN)] = h.astype(BF16)
            w_start(q + kk + 2)

    def s0_copy(u, c, k, j):
        s1, s2, _ = bits(k)
        i1 = jnp.where(j < 2, 1 - s1, s1)
        i2 = jnp.where(lax.rem(j, 2) == 0, 1 - s2, s2)
        i = i1 * 2 + i2
        slot = lax.rem(u, 3)
        return pltpu.make_async_remote_copy(
            st0.at[slot], rv0.at[k, i], s0s.at[slot], r0.at[k, i], **to(core_peer))

    def r0_wait(k, i):
        pltpu.make_async_remote_copy(st0.at[0], rv0.at[k, i], s0s.at[0], r0.at[k, i], **to(core_peer)).wait_recv()

    def s0(c, u0, j0, step0):
        def body(t, _):
            k, j = t // 2, j0 + lax.rem(t, 2)
            u = c * 12 + u0 + t
            slot = d_next(step0 + t)
            y = jnp.dot(hv[lax.rem(c, 2)], dbuf[slot], preferred_element_type=F32)

            @pl.when(u >= 3)
            def _():
                s0_copy(u, c, k, j).wait_send()

            st0[lax.rem(u, 3)] = y.astype(BF16)
            s0_copy(u, c, k, j).start()
            return 0

        lax.fori_loop(0, 6, body, 0)

    def s1_copy(k, j):
        s1, s2, _ = bits(k)
        i2 = jnp.where(j == 0, 1 - s2, s2)
        return pltpu.make_async_remote_copy(
            st1.at[k, j], rv1.at[k, i2], s1s.at[k, j], r1.at[k, i2], **to(peer(dim(k, 0))))

    def r1_wait(k, i2):
        pltpu.make_async_remote_copy(
            st1.at[k, 0], rv1.at[k, i2], s1s.at[k, 0], r1.at[k, i2], **to(peer(dim(k, 0)))).wait_recv()

    def s1(c, step0):
        def body(t, _):
            k, j = t // 2, lax.rem(t, 2)
            b1, b2, _ = bits(k)
            i2 = jnp.where(j == 0, 1 - b2, b2)
            i = (1 - b1) * 2 + i2
            slot = d_next(step0 + t)
            y = jnp.dot(hv[lax.rem(c, 2)], dbuf[slot], preferred_element_type=F32)
            r0_wait(k, i)

            @pl.when(c > 0)
            def _():
                s1_copy(k, j).wait_send()

            st1[k, j] = (y + rv0[k, i].astype(F32)).astype(BF16)
            s1_copy(k, j).start()
            return 0

        lax.fori_loop(0, 6, body, 0)

    def s2_copy(k):
        return pltpu.make_async_remote_copy(
            st2.at[k], rv2.at[k], s2s.at[k], r2.at[k], **to(peer(dim(k, 1))))

    def s2(c):
        def body(k, _):
            b1, b2, _ = bits(k)
            i = b1 * 2 + 1 - b2
            slot = d_next(c * WD_STEPS + 18 + k)
            y = jnp.dot(hv[lax.rem(c, 2)], dbuf[slot], preferred_element_type=F32)
            r0_wait(k, i)
            r1_wait(k, 1 - b2)

            @pl.when(c > 0)
            def _():
                s2_copy(k).wait_send()

            st2[k] = (y + rv0[k, i].astype(F32) + rv1[k, 1 - b2].astype(F32)).astype(BF16)
            s2_copy(k).start()
            return 0

        lax.fori_loop(0, 3, body, 0)

    def s3_copy(k):
        return pltpu.make_async_remote_copy(
            st3.at[k], rv3.at[k], s3s.at[k], r3.at[k], **to(peer(dim(k, 2))))

    def held(k, half):
        b1, b2, _ = bits(k)
        part = pl.ds(pl.multiple_of(half * HALF, HALF), HALF)
        return (rv0[k, b1 * 2 + b2, part].astype(F32) + rv1[k, b2, part].astype(F32)
                + rv2[k, part].astype(F32))

    def s3(c):
        def body(k, _):
            b1, b2, b3 = bits(k)
            slot = d_next(c * WD_STEPS + 21 + k)
            part = pl.ds(pl.multiple_of((1 - b3) * HALF, HALF), HALF)
            y = jnp.dot(hv[lax.rem(c, 2), part], dbuf[slot], preferred_element_type=F32)
            r0_wait(k, b1 * 2 + b2)
            r1_wait(k, b2)
            s2_copy(k).wait_recv()

            @pl.when(c > 0)
            def _():
                s3_copy(k).wait_send()

            st3[k] = (y + held(k, 1 - b3)).astype(BF16)
            s3_copy(k).start()
            return 0

        lax.fori_loop(0, 3, body, 0)

    def place(c, k, i1, i2, half):
        return y_hbm.at[pl.ds(pl.multiple_of(c * R + half * HALF, HALF), HALF), pl.ds(col(k, b0, i1, i2), CB)]

    def f_copies(c, k):
        b1, b2, b3 = bits(k)
        par = lax.rem(c, 2)
        dst = place(c, k, b1, b2, b3)
        return [
            pltpu.make_async_remote_copy(stf.at[k], dst, fs.at[k, 0], g3.at[par, k], **to(peer(dim(k, 2)))),
            pltpu.make_async_remote_copy(stf.at[k], dst, fs.at[k, 1], g2.at[par, k, 0], **to(peer(dim(k, 1)))),
            pltpu.make_async_remote_copy(stf.at[k], dst, fs.at[k, 2], g1.at[par, k, 0], **to(peer(dim(k, 0)))),
            pltpu.make_async_remote_copy(stf.at[k], dst, fs.at[k, 3], g0.at[c, k], **to(core_peer)),
        ]

    def f_local(c, k):
        b1, b2, b3 = bits(k)
        return pltpu.make_async_copy(stf.at[k], place(c, k, b1, b2, b3), fl.at[k])

    def f_wait(c):
        def body(k, _):
            f_local(c, k).wait()
            for cp in f_copies(c, k):
                cp.wait_send()
            return 0

        lax.fori_loop(0, 3, body, 0)

    def fin(c):
        @pl.when(c > 0)
        def _():
            f_wait(c - 1)

        def body(k, _):
            b1, b2, b3 = bits(k)
            slot = d_next(c * WD_STEPS + 24 + k)
            part = pl.ds(pl.multiple_of(b3 * HALF, HALF), HALF)
            y = jnp.dot(hv[lax.rem(c, 2), part], dbuf[slot], preferred_element_type=F32)
            s3_copy(k).wait_recv()
            stf[k] = (y + held(k, b3) + rv3[k].astype(F32)).astype(BF16)
            for cp in f_copies(c, k):
                cp.start()
            f_local(c, k).start()
            return 0

        lax.fori_loop(0, 3, body, 0)

        @pl.when(c < nc - 1)
        def _():
            for i, dev in enumerate(everyone):
                pl.semaphore_signal(credit.at[i], inc=1, **to(dev))

    def a3_copies(c, k):
        b1, b2, b3 = bits(k)
        par = lax.rem(c, 2)
        p = place(c, k, b1, b2, 1 - b3)
        return [
            pltpu.make_async_remote_copy(p, p, a3s.at[k, 0], g2.at[par, k, 1], **to(peer(dim(k, 1)))),
            pltpu.make_async_remote_copy(p, p, a3s.at[k, 1], g1.at[par, k, 1], **to(peer(dim(k, 0)))),
            pltpu.make_async_remote_copy(p, p, a3s.at[k, 2], g0.at[c, k], **to(core_peer)),
        ]

    def a2_copies(c, k, i):
        b1, b2, b3 = bits(k)
        par = lax.rem(c, 2)
        p = place(c, k, b1, 1 - b2, b3 if i == 0 else 1 - b3)
        return [
            pltpu.make_async_remote_copy(p, p, a2s.at[k, i, 0], g1.at[par, k, 2 + i], **to(peer(dim(k, 0)))),
            pltpu.make_async_remote_copy(p, p, a2s.at[k, i, 1], g0.at[c, k], **to(core_peer)),
        ]

    def a1_copies(c, k, i):
        b1, b2, b3 = bits(k)
        p = place(c, k, 1 - b1, b2 if i < 2 else 1 - b2, b3 if i % 2 == 0 else 1 - b3)
        return [pltpu.make_async_remote_copy(p, p, a1s.at[k, i], g0.at[c, k], **to(core_peer))]

    def landed(sem, p):
        pltpu.make_async_remote_copy(p, p, a1s.at[0, 0], sem, **to(core_peer)).wait_recv()

    def a3_wait(c):
        def body(k, _):
            for cp in a3_copies(c, k):
                cp.wait_send()
            return 0

        lax.fori_loop(0, 3, body, 0)

    def a3(c):
        @pl.when(c > 0)
        def _():
            a3_wait(c - 1)

        def body(k, _):
            b1, b2, b3 = bits(k)
            landed(g3.at[lax.rem(c, 2), k], place(c, k, b1, b2, 1 - b3))
            for cp in a3_copies(c, k):
                cp.start()
            return 0

        lax.fori_loop(0, 3, body, 0)

    def a2_wait(c):
        def body(k, _):
            for i in range(2):
                for cp in a2_copies(c, k, i):
                    cp.wait_send()
            return 0

        lax.fori_loop(0, 3, body, 0)

    def a2(c):
        @pl.when(c > 0)
        def _():
            a2_wait(c - 1)

        for i in range(2):
            def body(k, _):
                b1, b2, b3 = bits(k)
                landed(g2.at[lax.rem(c, 2), k, i], place(c, k, b1, 1 - b2, b3 if i == 0 else 1 - b3))
                for cp in a2_copies(c, k, i):
                    cp.start()
                return 0

            lax.fori_loop(0, 3, body, 0)

    def a1_wait(c):
        def body(k, _):
            for i in range(4):
                for cp in a1_copies(c, k, i):
                    cp.wait_send()
            return 0

        lax.fori_loop(0, 3, body, 0)

    def a1(c):
        @pl.when(c > 0)
        def _():
            a1_wait(c - 1)

        for i in range(4):
            def body(k, _):
                b1, b2, b3 = bits(k)
                landed(g1.at[lax.rem(c, 2), k, i],
                       place(c, k, 1 - b1, b2 if i < 2 else 1 - b2, b3 if i % 2 == 0 else 1 - b3))
                for cp in a1_copies(c, k, i):
                    cp.start()
                return 0

            lax.fori_loop(0, 3, body, 0)

    def a0_wait(c):
        def body(k, _):
            p = y_hbm.at[pl.ds(pl.multiple_of(c * R, R), R), pl.ds(col(k, 1 - b0, 0, 0), 4 * CB)]
            landed(g0.at[c, k], p)
            return 0

        lax.fori_loop(0, 3, body, 0)

    def chunk(c, _):
        @pl.when(c < nc)
        def _():
            for cp in x_copies(c):
                cp.wait()

        def tile(n, _):
            @pl.when(c < nc)
            def _():
                gate_up(c, n)

            @pl.when((n == 0) & (c >= 2))
            def _():
                a1(c - 2)

            late = (c >= 1) & (c <= nc)
            for slot, act in SLOTS:
                @pl.when(late & (n == slot))
                def _(act=act):
                    {"s2": s2, "s3": s3, "fin": fin, "a3": a3, "a2": a2}[act](c - 1)

            return 0

        lax.fori_loop(0, nt, tile, 0)

        @pl.when(c < nc)
        def _():
            @pl.when(c < nc - 1)
            def _():
                for cp in x_copies(c + 1):
                    cp.start()

            @pl.when(c > 0)
            def _():
                for i in range(4):
                    pl.semaphore_wait(credit.at[i], 1)

            s0(c, 0, 0, c * WD_STEPS)
            s1(c, c * WD_STEPS + 6)
            s0(c, 6, 2, c * WD_STEPS + 12)

        return 0

    lax.fori_loop(0, nc + 2, chunk, 0)

    last = nc - 1
    for slot in range(3):
        s0_copy(slot, last, 0, 0).wait_send()

    def drain(k, _):
        for j in range(2):
            s1_copy(k, j).wait_send()
        s2_copy(k).wait_send()
        s3_copy(k).wait_send()
        return 0

    lax.fori_loop(0, 3, drain, 0)
    f_wait(last)
    a3_wait(last)
    a2_wait(last)
    a1_wait(last)

    def land(c, _):
        a0_wait(c)
        return 0

    lax.fori_loop(0, nc, land, 0)


SLOTS = ((1, "s2"), (2, "s3"), (3, "fin"), (5, "a3"), (6, "a2"))


def block(x, wg, wu, wd):
    rows, depth = x.shape
    units = wg.shape[1]
    nc = rows // R
    dma, vmem = pltpu.SemaphoreType.DMA, pltpu.VMEM
    return pl.pallas_call(
        kernel,
        name="mlp",
        out_shape=jax.ShapeDtypeStruct((rows, depth), BF16),
        in_specs=[pl.BlockSpec(memory_space=pl.ANY)] * 4,
        out_specs=pl.BlockSpec(memory_space=pl.ANY),
        scratch_shapes=[
            vmem((2, R, KB), BF16),
            vmem((2, KB, 2 * GN), BF16),
            vmem((R, 2 * GN), F32),
            vmem((2, R, units), BF16),
            vmem((3, units, CB), BF16),
            vmem((3, 4, R, CB), BF16),
            vmem((3, 2, R, CB), BF16),
            vmem((3, R, CB), BF16),
            vmem((3, HALF, CB), BF16),
            vmem((3, R, CB), BF16),
            vmem((3, 2, R, CB), BF16),
            vmem((3, R, CB), BF16),
            vmem((3, HALF, CB), BF16),
            vmem((3, HALF, CB), BF16),
            dma((2,)), dma((2, 2)), dma((3,)),
            dma((3,)), dma((3, 2)), dma((3,)), dma((3,)), dma((3, 4)), dma((3,)), dma((3, 3)), dma((3, 2, 2)), dma((3, 4)),
            dma((3, 4)), dma((3, 2)), dma((3,)), dma((3,)),
            dma((2, 3)), dma((2, 3, 2)), dma((2, 3, 4)), dma((nc, 3)),
            pltpu.SemaphoreType.REGULAR((4,)),
        ],
        compiler_params=pltpu.CompilerParams(
            collective_id=0, has_side_effects=True, vmem_limit_bytes=67_043_328
        ),
    )(x, wg, wu, wd)


def solution(mesh):
    return jax.shard_map(
        block,
        mesh=mesh,
        in_specs=(P("dp", None), P(None, "tp"), P(None, "tp"), P("tp", None)),
        out_specs=P("dp", None),
        check_vma=False,
    )
```

time: 810 us -> 475 us (0.59)
  waiting for transfers between devices: 456 us -> 0 us
  Pallas kernels: 0 us -> 441 us
  matrix products: 307 us -> 0 us
  between operations: 13.4 us -> 0.01 us
    psum x1 -> x0, waiting for transfers between devices: 456 us -> none  [step(): return lax.psum(term, 'tp')]
    pallas_call x0 -> x1, Pallas kernels: none -> 441 us  [block(): pl.pallas_call(kernel, name='mlp', out_shape=jax.ShapeDtypeStruct((rows,...]
    dot_general x3 -> x0, matrix products: 307 us -> none  [the longest x1 105 us: step(): up = jnp.dot(x, w_up, preferred_element_type=jnp.float32)]
  transfers between devices with their start and end apart: 1 -> 0, of which waited for: 1 -> 0; matrix products, arithmetic and copies ran while one was open for 0% -> 0% of each run, Pallas kernels for 0% -> 0%
where the time goes in v1:
time: 475 us
  Pallas kernels  441 us (93%)
  local copies, waits for them, and re-layouts  33.7 us (7%)
    pallas_call x1, Pallas kernels, block(): pl.pallas_call(kernel, name='mlp', out_shape=jax.ShapeDtypeStruct((rows,...  441 us
    unnamed x1, local copies, waits for them, and re-layouts  33.7 us

profile of v1, /device:TPU:0, one launch (start us, length us, event | category | flops | bytes accessed | tf_op | source)
XLA Modules:
  0.0 474.6 jit_solution(6697136312822075478)
XLA Ops:
  0.0 440.9 %mlp.1 = bf16[2048,12288]{1,0:T(8,128)(2,1)} custom-call(bf16[2048,12288]{1,0:T(8,128)(2,1)} %x_hbm.1, bf16[12288,1792]{1,0:T(8,128)(2,1)} %wg_hbm.1, bf16[12288,1792]{1,0:T(8,128)(2,1)} %wu_hbm.1, bf16[1792,12288]{1,0:T(8,128)(2,1)} %wd_hbm.1), custom_call_target="tpu_custom_call" | custom-call | tf_op jit(solution)/shard_map/mlp/pallas_call | solution.py:478
  440.9 33.7 %copy.6 = bf16[2048,12288]{1,0:T(8,128)(2,1)} copy(bf16[2048,12288]{1,0:T(8,128)(2,1)} %mlp.1) | data formatting | bytes 100663296

commit v2 on v0

v2 whole, which is shorter than its diff:
```python
import jax
import jax.numpy as jnp
from jax import lax
from jax.experimental import pallas as pl
from jax.experimental.pallas import tpu as pltpu
from jax.sharding import PartitionSpec as P

MESH = pl.DeviceIdType.MESH
F32, BF16 = jnp.float32, jnp.bfloat16

BIG = 352
CB = 512
PACKETS = 2
W_SLOTS = 3
GN = 256
D_STEPS = 12

SLOTS = ((0, "s2", 1), (1, "a3", 2), (3, "s3", 1), (4, "a2", 2), (5, "fin", 1), (6, "a1", 2))


def kernel(x_hbm, wg_hbm, wu_hbm, wd_hbm, y_hbm,
           xv, wbuf, acc, hv, dbuf, rv0, rv1, rv2, rv3, st, st3, stf,
           x_sem, w_sem, d_sem, s0s, s1s, s2s, s3s, fs, fl, a3s, a2s, a1s,
           r0, r1, r2, r3, g3, g2, g1, g0, credit):
    rows, depth = x_hbm.shape
    units = wg_hbm.shape[1]
    kb = depth // PACKETS
    nt = units // GN
    nb = rows // BIG
    nc = nb + 1
    me = lax.axis_index("tp")
    b0 = lax.rem(me, 2)

    def mask(d):
        return jnp.where(d == 0, 8, jnp.where(d == 1, 4, 2))

    def bit(d):
        return lax.rem(me // mask(d), 2)

    def peer(d):
        m = mask(d)
        return me + m - 2 * m * bit(d)

    core_peer = me + 1 - 2 * b0

    def dim(k, s):
        return lax.rem(k + s, 3)

    def bits(k):
        return bit(dim(k, 0)), bit(dim(k, 1)), bit(dim(k, 2))

    def col(k, i0, i1, i2):
        return pl.multiple_of((k * 8 + i0 * 4 + i1 * 2 + i2) * CB, CB)

    def to(dev):
        return dict(device_id={"tp": dev}, device_id_type=MESH)

    def loop(n, body):
        def step(i, _):
            body(i)
            return 0

        lax.fori_loop(0, n, step, 0)

    def w_copies(q):
        n, kk, slot = lax.rem(q // PACKETS, nt), lax.rem(q, PACKETS), lax.rem(q, W_SLOTS)
        src = (pl.ds(pl.multiple_of(kk * kb, kb), kb), pl.ds(pl.multiple_of(n * GN, GN), GN))
        return [
            pltpu.make_async_copy(wg_hbm.at[src], wbuf.at[slot, :, pl.ds(0, GN)], w_sem.at[slot, 0]),
            pltpu.make_async_copy(wu_hbm.at[src], wbuf.at[slot, :, pl.ds(GN, GN)], w_sem.at[slot, 1]),
        ]

    def w_next(q):
        for cp in w_copies(q):
            cp.wait()

        @pl.when(q + W_SLOTS - 1 < nc * nt * PACKETS)
        def _():
            for cp in w_copies(q + W_SLOTS - 1):
                cp.start(priority=1)

        return lax.rem(q, W_SLOTS)

    def d_copy(step):
        r, slot = lax.rem(step, D_STEPS), lax.rem(step, 3)
        k, group = lax.rem(r, 3), r // 3
        b1, _, _ = bits(k)
        i0 = jnp.where((group == 0) | (group == 2), 1 - b0, b0)
        i1 = jnp.where(group < 2, 1 - b1, b1)
        return pltpu.make_async_copy(
            wd_hbm.at[:, pl.ds(pl.multiple_of(col(k, i0, i1, 0), 2 * CB), 2 * CB)], dbuf.at[slot], d_sem.at[slot])

    def d_next(step):
        d_copy(step).wait()
        d_copy(step + 2).start()
        return lax.rem(step, 3)

    class Chunk:
        def __init__(self, R):
            self.R, self.half = R, R // 2

        def x_copy(self, c, i):
            return pltpu.make_async_copy(
                x_hbm.at[pl.ds(pl.multiple_of(c * BIG, 32), self.R), pl.ds(i * kb, kb)],
                xv.at[i, pl.ds(0, self.R)], x_sem.at[i])

        def gu_epilogue(self, c, n):
            t = acc[pl.ds(0, self.R)]
            h = jax.nn.silu(t[:, :GN]) * t[:, GN:]
            hv[lax.rem(c, 2), pl.ds(0, self.R), pl.ds(pl.multiple_of(n * GN, GN), GN)] = h.astype(BF16)

        def gate_up(self, c, n):
            for i in range(PACKETS):
                pl.when(n == 0)(lambda i=i: self.x_copy(c, i).wait())
                slot = w_next((c * nt + n) * PACKETS + i)
                if i == 0:
                    self.gu_epilogue(c, lax.rem(n + nt - 1, nt))
                d = jnp.dot(xv[i, pl.ds(0, self.R)], wbuf[slot], preferred_element_type=F32)
                acc[pl.ds(0, self.R)] = d if i == 0 else acc[pl.ds(0, self.R)] + d
                pl.when(n == nt - 1)(lambda i=i: either(c + 1, lambda a: a.x_copy(c + 1, i).start(priority=1)))

        def down(self, c, slot, i2, row, n):
            return jnp.dot(hv[lax.rem(c, 2), pl.ds(row, n)],
                           dbuf[slot, :, pl.ds(pl.multiple_of(i2 * CB, CB), CB)], preferred_element_type=F32)

        def pairs(self, c, step0, ready, sums, staged, send):
            def pair(k):
                slot = d_next(step0 + k)
                _, b2, _ = bits(k)
                ready(k)
                for j in range(2):
                    y = self.down(c, slot, 1 - b2 if j == 0 else b2, 0, self.R)
                    for a in sums(k, j):
                        y = y + a[pl.ds(0, self.R)].astype(F32)
                    st[staged(k, j), pl.ds(0, self.R)] = y.astype(BF16)
                for j in range(2):
                    send(k, j)

            loop(3, pair)

        def whole(self, ref):
            return ref.at[pl.ds(0, self.R)]

        def s0_copy(self, p, k, first, j):
            b1, b2, _ = bits(k)
            i1 = 1 - b1 if first else b1
            i, slot = i1 * 2 + (1 - b2 if j == 0 else b2), lax.rem(p, 2) * 2 + j
            return pltpu.make_async_remote_copy(
                self.whole(st.at[slot]), self.whole(rv0.at[k, i]), s0s.at[slot], r0.at[k, i], **to(core_peer))

        def r0_wait(self, k, i):
            pltpu.make_async_remote_copy(
                self.whole(st.at[0]), self.whole(rv0.at[k, i]), s0s.at[0], r0.at[k, i], **to(core_peer)).wait_recv()

        def s0(self, c, first):
            p0 = 0 if first else 3

            def ready(k):
                def wait(chunk):
                    for j in range(2):
                        chunk.s0_copy(p0 + k, k, first, j).wait_send()

                if first:
                    pl.when(k == 2)(lambda: wait(self))
                    pl.when((k < 2) & (c > 0))(lambda: wait(big))
                else:
                    wait(self)

            self.pairs(c, c * D_STEPS + 2 * p0, ready, lambda k, j: [], lambda k, j: lax.rem(p0 + k, 2) * 2 + j,
                       lambda k, j: self.s0_copy(p0 + k, k, first, j).start())

        def s1_copy(self, k, j):
            _, b2, _ = bits(k)
            i2 = 1 - b2 if j == 0 else b2
            return pltpu.make_async_remote_copy(
                self.whole(st.at[4 + k * 2 + j]), self.whole(rv1.at[k, i2]), s1s.at[k, j], r1.at[k, i2],
                **to(peer(dim(k, 0))))

        def r1_wait(self, k, i2):
            pltpu.make_async_remote_copy(
                self.whole(st.at[4]), self.whole(rv1.at[k, i2]), s1s.at[k, 0], r1.at[k, i2],
                **to(peer(dim(k, 0)))).wait_recv()

        def s1(self, c):
            def index(k, j):
                b1, b2, _ = bits(k)
                return (1 - b1) * 2 + (1 - b2 if j == 0 else b2)

            def ready(k):
                for j in range(2):
                    self.r0_wait(k, index(k, j))
                    pl.when(c > 0)(lambda j=j: big.s1_copy(k, j).wait_send())

            self.pairs(c, c * D_STEPS + 3, ready, lambda k, j: [rv0.at[k, index(k, j)]],
                       lambda k, j: 4 + k * 2 + j, lambda k, j: self.s1_copy(k, j).start())

        def s2_copy(self, k):
            return pltpu.make_async_remote_copy(
                self.whole(st.at[10 + k]), self.whole(rv2.at[k]), s2s.at[k], r2.at[k], **to(peer(dim(k, 1))))

        def s2(self, c):
            def body(k):
                b1, b2, _ = bits(k)
                i = b1 * 2 + 1 - b2
                step = c * D_STEPS + 9 + k
                d_copy(step).wait()
                pl.when(k == 0)(lambda: d_copy(step + 2).start())
                self.r0_wait(k, i)
                self.r1_wait(k, 1 - b2)
                pl.when(c > 0)(lambda: big.s2_copy(k).wait_send())
                y = self.down(c, k, 1 - b2, 0, self.R)
                for a in (rv0.at[k, i], rv1.at[k, 1 - b2]):
                    y = y + a[pl.ds(0, self.R)].astype(F32)
                st[10 + k, pl.ds(0, self.R)] = y.astype(BF16)
                self.s2_copy(k).start()

            loop(3, body)

        def last(self, c, k, part, more, dst):
            b1, b2, _ = bits(k)
            row = pl.multiple_of(part * self.half, 16)
            y = self.down(c, k, b2, row, self.half)
            for a in (rv0.at[k, b1 * 2 + b2], rv1.at[k, b2], rv2.at[k]):
                y = y + a[pl.ds(row, self.half)].astype(F32)
            if more:
                y = y + rv3[k, pl.ds(0, self.half)].astype(F32)
            dst[k, pl.ds(0, self.half)] = y.astype(BF16)

        def s3_copy(self, k):
            n = pl.ds(0, self.half)
            return pltpu.make_async_remote_copy(
                st3.at[k, n], rv3.at[k, n], s3s.at[k], r3.at[k], **to(peer(dim(k, 2))))

        def s3(self, c):
            def body(k):
                b1, b2, b3 = bits(k)
                self.r0_wait(k, b1 * 2 + b2)
                self.r1_wait(k, b2)
                self.s2_copy(k).wait_recv()
                pl.when(c > 0)(lambda: big.s3_copy(k).wait_send())
                self.last(c, k, 1 - b3, False, st3)
                self.s3_copy(k).start()

            loop(3, body)

        def place(self, c, k, i1, i2, part):
            row = pl.multiple_of(c * BIG + part * self.half, 16)
            return y_hbm.at[pl.ds(row, self.half), pl.ds(col(k, b0, i1, i2), CB)]

        def f_copies(self, c, k):
            b1, b2, b3 = bits(k)
            par = lax.rem(c, 2)
            src, dst = stf.at[k, pl.ds(0, self.half)], self.place(c, k, b1, b2, b3)
            return [
                pltpu.make_async_remote_copy(src, dst, fs.at[k, 0], g3.at[par, k], **to(peer(dim(k, 2)))),
                pltpu.make_async_remote_copy(src, dst, fs.at[k, 1], g2.at[par, k, 0], **to(peer(dim(k, 1)))),
                pltpu.make_async_remote_copy(src, dst, fs.at[k, 2], g1.at[par, k, 0], **to(peer(dim(k, 0)))),
                pltpu.make_async_remote_copy(src, dst, fs.at[k, 3], g0.at[c, k], **to(core_peer)),
                pltpu.make_async_copy(src, dst, fl.at[k]),
            ]

        def f_wait(self, c):
            def body(k):
                copies = self.f_copies(c, k)
                for cp in copies[:4]:
                    cp.wait_send()
                copies[4].wait()

            loop(3, body)

        def fin(self, c):
            pl.when(c > 0)(lambda: big.f_wait(c - 1))

            def body(k):
                _, _, b3 = bits(k)
                self.s3_copy(k).wait_recv()
                self.last(c, k, b3, True, stf)
                copies = self.f_copies(c, k)
                copies[0].start()
                copies[4].start()
                pl.when((k < 2) & (c < nc - 1))(lambda: d_copy((c + 1) * D_STEPS + k).start())

            loop(3, body)
            for i in (1, 2, 3):
                loop(3, lambda k, i=i: self.f_copies(c, k)[i].start())

            @pl.when(c < nc - 1)
            def _():
                for i, dev in enumerate(everyone):
                    pl.semaphore_signal(credit.at[i], inc=1, **to(dev))

        def a3_copies(self, c, k):
            b1, b2, b3 = bits(k)
            par = lax.rem(c, 2)
            p = self.place(c, k, b1, b2, 1 - b3)
            return [
                pltpu.make_async_remote_copy(p, p, a3s.at[k, 0], g2.at[par, k, 1], **to(peer(dim(k, 1)))),
                pltpu.make_async_remote_copy(p, p, a3s.at[k, 1], g1.at[par, k, 1], **to(peer(dim(k, 0)))),
                pltpu.make_async_remote_copy(p, p, a3s.at[k, 2], g0.at[c, k], **to(core_peer)),
            ]

        def a2_copies(self, c, k, i):
            b1, b2, b3 = bits(k)
            par = lax.rem(c, 2)
            p = self.place(c, k, b1, 1 - b2, b3 if i == 0 else 1 - b3)
            return [
                pltpu.make_async_remote_copy(p, p, a2s.at[k, i, 0], g1.at[par, k, 2 + i], **to(peer(dim(k, 0)))),
                pltpu.make_async_remote_copy(p, p, a2s.at[k, i, 1], g0.at[c, k], **to(core_peer)),
            ]

        def a1_copies(self, c, k, i):
            b1, b2, b3 = bits(k)
            p = self.place(c, k, 1 - b1, b2 if i < 2 else 1 - b2, b3 if i % 2 == 0 else 1 - b3)
            return [pltpu.make_async_remote_copy(p, p, a1s.at[k, i], g0.at[c, k], **to(core_peer))]

        def landed(self, sem, p):
            pltpu.make_async_remote_copy(p, p, a1s.at[0, 0], sem, **to(core_peer)).wait_recv()

        def sent(self, c, copies):
            def body(k):
                for cp in copies(c, k):
                    cp.wait_send()

            loop(3, body)

        def a3_wait(self, c):
            self.sent(c, self.a3_copies)

        def a2_wait(self, c):
            self.sent(c, lambda c, k: self.a2_copies(c, k, 0) + self.a2_copies(c, k, 1))

        def a1_wait(self, c):
            self.sent(c, lambda c, k: sum((self.a1_copies(c, k, i) for i in range(4)), []))

        def a3(self, c):
            pl.when(c > 0)(lambda: big.a3_wait(c - 1))

            def body(k):
                b1, b2, b3 = bits(k)
                self.landed(g3.at[lax.rem(c, 2), k], self.place(c, k, b1, b2, 1 - b3))
                for cp in self.a3_copies(c, k):
                    cp.start()

            loop(3, body)

        def a2(self, c):
            pl.when(c > 0)(lambda: big.a2_wait(c - 1))
            for i in range(2):
                def body(k, i=i):
                    b1, b2, b3 = bits(k)
                    self.landed(g2.at[lax.rem(c, 2), k, i], self.place(c, k, b1, 1 - b2, b3 if i == 0 else 1 - b3))
                    for cp in self.a2_copies(c, k, i):
                        cp.start()

                loop(3, body)

        def a1(self, c):
            pl.when(c > 0)(lambda: big.a1_wait(c - 1))
            for i in range(4):
                def body(k, i=i):
                    b1, b2, b3 = bits(k)
                    self.landed(g1.at[lax.rem(c, 2), k, i],
                                self.place(c, k, 1 - b1, b2 if i < 2 else 1 - b2, b3 if i % 2 == 0 else 1 - b3))
                    for cp in self.a1_copies(c, k, i):
                        cp.start()

                loop(3, body)

        def a0_wait(self, c):
            def body(k):
                p = y_hbm.at[pl.ds(pl.multiple_of(c * BIG, 32), self.R), pl.ds(col(k, 1 - b0, 0, 0), 4 * CB)]
                self.landed(g0.at[c, k], p)

            loop(3, body)

        def early(self, c):
            self.gu_epilogue(c, nt - 1)

            @pl.when(c > 0)
            def _():
                for i in range(4):
                    pl.semaphore_wait(credit.at[i], 1)

            self.s0(c, True)
            self.s1(c)
            self.s0(c, False)

    big, small = Chunk(BIG), Chunk(rows - nb * BIG)

    def either(c, act):
        pl.when((c >= 0) & (c < nb))(lambda: act(big))
        pl.when(c == nb)(lambda: act(small))

    for i in range(PACKETS):
        for cp in w_copies(i):
            cp.start()
        big.x_copy(0, i).start()
    d_copy(0).start()
    d_copy(1).start()

    barrier = pltpu.get_barrier_semaphore()
    everyone = [peer(0), peer(1), peer(2), core_peer]
    for dev in everyone:
        pl.semaphore_signal(barrier, inc=1, **to(dev))
    pl.semaphore_wait(barrier, 4)

    def chunk(c):
        def tile(n):
            either(c, lambda a: a.gate_up(c, n))
            for slot, act, lag in SLOTS:
                pl.when(n == slot)(lambda act=act, lag=lag: either(c - lag, lambda a: getattr(a, act)(c - lag)))

        loop(nt, tile)
        either(c, lambda a: a.early(c))

    loop(nc + 2, chunk)

    last = nc - 1
    for k in (1, 2):
        for j in range(2):
            small.s0_copy(3 + k, k, False, j).wait_send()

    def drain(k):
        for j in range(2):
            small.s1_copy(k, j).wait_send()
        small.s2_copy(k).wait_send()
        small.s3_copy(k).wait_send()

    loop(3, drain)
    small.f_wait(last)
    small.a3_wait(last)
    small.a2_wait(last)
    small.a1_wait(last)
    loop(nc, lambda c: either(c, lambda a: a.a0_wait(c)))


def block(x, wg, wu, wd):
    rows, depth = x.shape
    units = wg.shape[1]
    nc = rows // BIG + 1
    kb = depth // PACKETS
    dma, vmem = pltpu.SemaphoreType.DMA, pltpu.VMEM
    return pl.pallas_call(
        kernel,
        name="mlp",
        out_shape=jax.ShapeDtypeStruct((rows, depth), BF16),
        in_specs=[pl.BlockSpec(memory_space=pl.ANY)] * 4,
        out_specs=pl.BlockSpec(memory_space=pl.ANY),
        scratch_shapes=[
            vmem((PACKETS, BIG, kb), BF16),
            vmem((W_SLOTS, kb, 2 * GN), BF16),
            vmem((BIG, 2 * GN), F32),
            vmem((2, BIG, units), BF16),
            vmem((3, units, 2 * CB), BF16),
            vmem((3, 4, BIG, CB), BF16),
            vmem((3, 2, BIG, CB), BF16),
            vmem((3, BIG, CB), BF16),
            vmem((3, BIG // 2, CB), BF16),
            vmem((13, BIG, CB), BF16),
            vmem((3, BIG // 2, CB), BF16),
            vmem((3, BIG // 2, CB), BF16),
            dma((PACKETS,)), dma((W_SLOTS, 2)), dma((3,)),
            dma((4,)), dma((3, 2)), dma((3,)), dma((3,)), dma((3, 4)), dma((3,)),
            dma((3, 3)), dma((3, 2, 2)), dma((3, 4)),
            dma((3, 4)), dma((3, 2)), dma((3,)), dma((3,)),
            dma((2, 3)), dma((2, 3, 2)), dma((2, 3, 4)), dma((nc, 3)),
            pltpu.SemaphoreType.REGULAR((4,)),
        ],
        compiler_params=pltpu.CompilerParams(
            collective_id=0, has_side_effects=True, vmem_limit_bytes=67_043_328
        ),
    )(x, wg, wu, wd)


def solution(mesh):
    return jax.shard_map(
        block,
        mesh=mesh,
        in_specs=(P("dp", None), P(None, "tp"), P(None, "tp"), P("tp", None)),
        out_specs=P("dp", None),
        check_vma=False,
    )
```

time: 810 us -> 432 us (0.53)
  waiting for transfers between devices: 456 us -> 0 us
  Pallas kernels: 0 us -> 398 us
  matrix products: 307 us -> 0 us
  between operations: 13.4 us -> 0.01 us
    psum x1 -> x0, waiting for transfers between devices: 456 us -> none  [step(): return lax.psum(term, 'tp')]
    pallas_call x0 -> x1, Pallas kernels: none -> 398 us  [block(): pl.pallas_call(kernel, name='mlp', out_shape=jax.ShapeDtypeStruct((rows,...]
    dot_general x3 -> x0, matrix products: 307 us -> none  [the longest x1 105 us: step(): up = jnp.dot(x, w_up, preferred_element_type=jnp.float32)]
  transfers between devices with their start and end apart: 1 -> 0, of which waited for: 1 -> 0; matrix products, arithmetic and copies ran while one was open for 0% -> 0% of each run, Pallas kernels for 0% -> 0%
where the time goes in v2:
time: 432 us
  Pallas kernels  398 us (92%)
  local copies, waits for them, and re-layouts  33.7 us (8%)
    pallas_call x1, Pallas kernels, block(): pl.pallas_call(kernel, name='mlp', out_shape=jax.ShapeDtypeStruct((rows,...  398 us
    unnamed x1, local copies, waits for them, and re-layouts  33.7 us

profile of v2, /device:TPU:0, one launch (start us, length us, event | category | flops | bytes accessed | tf_op | source)
XLA Modules:
  0.0 432.2 jit_solution(1532940354820972741)
XLA Ops:
  0.0 398.5 %mlp.1 = bf16[2048,12288]{1,0:T(8,128)(2,1)} custom-call(bf16[2048,12288]{1,0:T(8,128)(2,1)} %x_hbm.1, bf16[12288,1792]{1,0:T(8,128)(2,1)} %wg_hbm.1, bf16[12288,1792]{1,0:T(8,128)(2,1)} %wu_hbm.1, bf16[1792,12288]{1,0:T(8,128)(2,1)} %wd_hbm.1), custom_call_target="tpu_custom_call" | custom-call | tf_op jit(solution)/shard_map/mlp/pallas_call | solution.py:443
  398.5 33.7 %copy.6 = bf16[2048,12288]{1,0:T(8,128)(2,1)} copy(bf16[2048,12288]{1,0:T(8,128)(2,1)} %mlp.1) | data formatting | bytes 100663296

commit v3 on v2

v3 whole, which is shorter than its diff:
```python
import jax
import jax.numpy as jnp
from jax import lax
from jax.experimental import pallas as pl
from jax.experimental.pallas import tpu as pltpu
from jax.sharding import PartitionSpec as P

MESH = pl.DeviceIdType.MESH
F32, BF16 = jnp.float32, jnp.bfloat16

BIG = 352
CB = 512
PACKETS = 2
W_SLOTS = 3
GN = 256
D_STEPS = 12

SLOTS = ((1, "s2", 1), (4, "s3", 1), (5, "a2", 2), (8, "fin", 1), (12, "a1", 2), (12, "a3", 1))


def kernel(x_hbm, wg_hbm, wu_hbm, wd_hbm, y_hbm,
           xv, wbuf, acc, hv, dbuf, raw, rv0, rv1, rv2, rv3, st, st3, stf,
           x_sem, w_sem, d_sem, s0s, s1s, s2s, s3s, fs, fl, a3s, a2s, a1s,
           r0, r1, r2, r3, g3, g2, g1, g0, credit):
    rows, depth = x_hbm.shape
    units = wg_hbm.shape[1]
    kb = depth // PACKETS
    nt = units // GN
    nb = rows // BIG
    nc = nb + 1
    me = lax.axis_index("tp")
    b0 = lax.rem(me, 2)

    def mask(d):
        return jnp.where(d == 0, 8, jnp.where(d == 1, 4, 2))

    def bit(d):
        return lax.rem(me // mask(d), 2)

    def peer(d):
        m = mask(d)
        return me + m - 2 * m * bit(d)

    core_peer = me + 1 - 2 * b0

    def dim(k, s):
        return lax.rem(k + s, 3)

    def bits(k):
        return bit(dim(k, 0)), bit(dim(k, 1)), bit(dim(k, 2))

    def col(k, i0, i1, i2):
        return pl.multiple_of((k * 8 + i0 * 4 + i1 * 2 + i2) * CB, CB)

    def to(dev):
        return dict(device_id={"tp": dev}, device_id_type=MESH)

    def loop(n, body):
        def step(i, _):
            body(i)
            return 0

        lax.fori_loop(0, n, step, 0)

    def w_copies(q):
        n, kk, slot = lax.rem(q // PACKETS, nt), lax.rem(q, PACKETS), lax.rem(q, W_SLOTS)
        src = (pl.ds(pl.multiple_of(kk * kb, kb), kb), pl.ds(pl.multiple_of(n * GN, GN), GN))
        return [
            pltpu.make_async_copy(wg_hbm.at[src], wbuf.at[slot, :, pl.ds(0, GN)], w_sem.at[slot, 0]),
            pltpu.make_async_copy(wu_hbm.at[src], wbuf.at[slot, :, pl.ds(GN, GN)], w_sem.at[slot, 1]),
        ]

    def w_next(q):
        for cp in w_copies(q):
            cp.wait()

        @pl.when(q + W_SLOTS - 1 < nc * nt * PACKETS)
        def _():
            for cp in w_copies(q + W_SLOTS - 1):
                cp.start(priority=1)

        return lax.rem(q, W_SLOTS)

    def d_copy(step):
        r, slot = lax.rem(step, D_STEPS), lax.rem(step, 3)
        k, group = lax.rem(r, 3), r // 3
        b1, _, _ = bits(k)
        i0 = jnp.where((group == 0) | (group == 2), 1 - b0, b0)
        i1 = jnp.where(group < 2, 1 - b1, b1)
        return pltpu.make_async_copy(
            wd_hbm.at[:, pl.ds(pl.multiple_of(col(k, i0, i1, 0), 2 * CB), 2 * CB)], dbuf.at[slot], d_sem.at[slot])

    def d_start(step):
        pl.when(step < nc * D_STEPS)(lambda: d_copy(step).start())

    class Chunk:
        def __init__(self, R):
            self.R, self.half = R, R // 2

        def x_copy(self, c, i):
            return pltpu.make_async_copy(
                x_hbm.at[pl.ds(pl.multiple_of(c * BIG, 32), self.R), pl.ds(i * kb, kb)],
                xv.at[i, pl.ds(0, self.R)], x_sem.at[i])

        def gu_epilogue(self, c, n):
            t = acc[pl.ds(0, self.R)]
            h = jax.nn.silu(t[:, :GN]) * t[:, GN:]
            hv[lax.rem(c, 2), pl.ds(0, self.R), pl.ds(pl.multiple_of(n * GN, GN), GN)] = h.astype(BF16)

        def gate_up(self, c, n, i):
            pl.when(n == 0)(lambda: self.x_copy(c, i).wait())
            slot = w_next((c * nt + n) * PACKETS + i)
            if i == 0:
                self.gu_epilogue(c, lax.rem(n + nt - 1, nt))
            d = jnp.dot(xv[i, pl.ds(0, self.R)], wbuf[slot], preferred_element_type=F32)
            acc[pl.ds(0, self.R)] = d if i == 0 else acc[pl.ds(0, self.R)] + d
            if i == 0:
                pl.when(n == nt - 1)(lambda: either(c + 1, lambda a: a.x_copy(c + 1, 0).start(priority=1)))

        def down(self, c, slot, i2):
            return jnp.dot(hv[lax.rem(c, 2), pl.ds(0, self.R)],
                           dbuf[slot, :, pl.ds(pl.multiple_of(i2 * CB, CB), CB)], preferred_element_type=F32)

        def pairs(self, c, step0, ready, sums, staged, send):
            def pair(k):
                _, b2, _ = bits(k)
                d_copy(step0 + k).wait()
                ready(k)
                both = jnp.dot(hv[lax.rem(c, 2), pl.ds(0, self.R)], dbuf[k], preferred_element_type=F32)
                for i2 in range(2):
                    j = jnp.where(b2 == i2, 1, 0)
                    y = both[:, i2 * CB : (i2 + 1) * CB]
                    for a in sums(k, i2):
                        y = y + a[pl.ds(0, self.R)].astype(F32)
                    st[staged(k, j), pl.ds(0, self.R)] = y.astype(BF16)
                for j in range(2):
                    send(k, j)
                d_start(step0 + k + 3)

            loop(3, pair)

        def whole(self, ref):
            return ref.at[pl.ds(0, self.R)]

        def s0_copy(self, k, first, j):
            b1, b2, _ = bits(k)
            i1 = 1 - b1 if first else b1
            i, slot = i1 * 2 + (1 - b2 if j == 0 else b2), k * 2 + j
            return pltpu.make_async_remote_copy(
                self.whole(st.at[slot]), self.whole(rv0.at[k, i]), s0s.at[slot], r0.at[k, i], **to(core_peer))

        def r0_wait(self, k, i):
            pltpu.make_async_remote_copy(
                self.whole(st.at[0]), self.whole(rv0.at[k, i]), s0s.at[0], r0.at[k, i], **to(core_peer)).wait_recv()

        def s0(self, c, first):
            def ready(k):
                def wait(chunk):
                    for j in range(2):
                        chunk.s0_copy(k, first, j).wait_send()

                if first:
                    pl.when(c > 0)(lambda: wait(big))
                else:
                    wait(self)

            self.pairs(c, c * D_STEPS + (0 if first else 6), ready, lambda k, i2: [], lambda k, j: k * 2 + j,
                       lambda k, j: self.s0_copy(k, first, j).start())

        def s1_copy(self, k, j):
            _, b2, _ = bits(k)
            i2 = 1 - b2 if j == 0 else b2
            return pltpu.make_async_remote_copy(
                self.whole(st.at[6 + k * 2 + j]), self.whole(rv1.at[k, i2]), s1s.at[k, j], r1.at[k, i2],
                **to(peer(dim(k, 0))))

        def r1_wait(self, k, i2):
            pltpu.make_async_remote_copy(
                self.whole(st.at[6]), self.whole(rv1.at[k, i2]), s1s.at[k, 0], r1.at[k, i2],
                **to(peer(dim(k, 0)))).wait_recv()

        def s1(self, c):
            def index(k, j):
                b1, b2, _ = bits(k)
                return (1 - b1) * 2 + (1 - b2 if j == 0 else b2)

            def ready(k):
                for j in range(2):
                    self.r0_wait(k, index(k, j))
                    pl.when(c > 0)(lambda j=j: big.s1_copy(k, j).wait_send())

            self.pairs(c, c * D_STEPS + 3, ready, lambda k, i2: [rv0.at[k, (1 - bits(k)[0]) * 2 + i2]],
                       lambda k, j: 6 + k * 2 + j, lambda k, j: self.s1_copy(k, j).start())

        def s2_copy(self, k, i):
            b3 = bits(k)[2]
            part = pl.ds(pl.multiple_of((1 - b3 if i == 0 else b3) * self.half, 16), self.half)
            return pltpu.make_async_remote_copy(
                st.at[12 + k, part], rv2.at[k, part], s2s.at[k, i], r2.at[k, i], **to(peer(dim(k, 1))))

        def s2(self, c):
            def body(k):
                b1, b2, _ = bits(k)
                i = b1 * 2 + 1 - b2
                step = c * D_STEPS + 9 + k
                d_copy(step).wait()
                self.r0_wait(k, i)
                self.r1_wait(k, 1 - b2)
                for j in range(2):
                    pl.when(c > 0)(lambda j=j: big.s2_copy(k, j).wait_send())
                y = self.down(c, k, 1 - b2)
                for a in (rv0.at[k, i], rv1.at[k, 1 - b2]):
                    y = y + a[pl.ds(0, self.R)].astype(F32)
                st[12 + k, pl.ds(0, self.R)] = y.astype(BF16)
                raw[k, pl.ds(0, self.R)] = self.down(c, k, b2)
                for i in range(2):
                    self.s2_copy(k, i).start()
                d_start(step + 3)

            loop(3, body)

        def last(self, k, part, more, dst):
            b1, b2, _ = bits(k)
            rows = pl.ds(pl.multiple_of(part * self.half, 16), self.half)
            y = raw[k, rows]
            for a in (rv0.at[k, b1 * 2 + b2], rv1.at[k, b2], rv2.at[k]):
                y = y + a[rows].astype(F32)
            if more:
                y = y + rv3[k, pl.ds(0, self.half)].astype(F32)
            dst[k, pl.ds(0, self.half)] = y.astype(BF16)

        def s3_copy(self, k):
            n = pl.ds(0, self.half)
            return pltpu.make_async_remote_copy(
                st3.at[k, n], rv3.at[k, n], s3s.at[k], r3.at[k], **to(peer(dim(k, 2))))

        def s3(self, c):
            def body(k):
                b1, b2, b3 = bits(k)
                self.r0_wait(k, b1 * 2 + b2)
                self.r1_wait(k, b2)
                self.s2_copy(k, 0).wait_recv()
                pl.when(c > 0)(lambda: big.s3_copy(k).wait_send())
                self.last(k, 1 - b3, False, st3)
                self.s3_copy(k).start()

            loop(3, body)

        def place(self, c, k, i1, i2, part):
            row = pl.multiple_of(c * BIG + part * self.half, 16)
            return y_hbm.at[pl.ds(row, self.half), pl.ds(col(k, b0, i1, i2), CB)]

        def f_copies(self, c, k):
            b1, b2, b3 = bits(k)
            par = lax.rem(c, 2)
            src, dst = stf.at[k, pl.ds(0, self.half)], self.place(c, k, b1, b2, b3)
            return [
                pltpu.make_async_remote_copy(src, dst, fs.at[k, 0], g3.at[par, k], **to(peer(dim(k, 2)))),
                pltpu.make_async_remote_copy(src, dst, fs.at[k, 1], g2.at[par, k, 0], **to(peer(dim(k, 1)))),
                pltpu.make_async_remote_copy(src, dst, fs.at[k, 2], g1.at[par, k, 0], **to(peer(dim(k, 0)))),
                pltpu.make_async_copy(src, dst, fl.at[k]),
            ]

        def f_wait(self, c):
            def body(k):
                copies = self.f_copies(c, k)
                for cp in copies[:3]:
                    cp.wait_send()

            loop(3, body)

        def fin(self, c):
            pl.when(c > 0)(lambda: big.f_wait(c - 1))

            def body(k):
                _, _, b3 = bits(k)
                self.s2_copy(k, 1).wait_recv()
                self.s3_copy(k).wait_recv()
                self.last(k, b3, True, stf)
                copies = self.f_copies(c, k)
                copies[0].start()
                copies[3].start()

            loop(3, body)
            for i in (1, 2):
                loop(3, lambda k, i=i: self.f_copies(c, k)[i].start())

            @pl.when(c < nc - 1)
            def _():
                for i, dev in enumerate(everyone):
                    pl.semaphore_signal(credit.at[i], inc=1, **to(dev))

        def part_of_y(self, c, col0, width):
            return y_hbm.at[pl.ds(pl.multiple_of(c * BIG, 32), self.R), pl.ds(col0, width)]

        def a3_copies(self, c, k):
            b1, b2, b3 = bits(k)
            par = lax.rem(c, 2)
            p = self.place(c, k, b1, b2, 1 - b3)
            return [
                pltpu.make_async_remote_copy(p, p, a3s.at[k, 0], g2.at[par, k, 1], **to(peer(dim(k, 1)))),
                pltpu.make_async_remote_copy(p, p, a3s.at[k, 1], g1.at[par, k, 1], **to(peer(dim(k, 0)))),
            ]

        def a2_copies(self, c, k):
            b1, b2, _ = bits(k)
            p = self.part_of_y(c, col(k, b0, b1, 1 - b2), CB)
            q = self.part_of_y(c, col(k, b0, b1, 0), 2 * CB)
            return [
                pltpu.make_async_remote_copy(p, p, a2s.at[k, 0], g1.at[lax.rem(c, 2), k, 2], **to(peer(dim(k, 0)))),
                pltpu.make_async_remote_copy(q, q, a2s.at[k, 1], g0.at[c, k, 0], **to(core_peer)),
            ]

        def a1_copies(self, c, k):
            b1, _, _ = bits(k)
            q = self.part_of_y(c, col(k, b0, 1 - b1, 0), 2 * CB)
            return [pltpu.make_async_remote_copy(q, q, a1s.at[k], g0.at[c, k, 1], **to(core_peer))]

        def landed(self, sem, p):
            pltpu.make_async_remote_copy(p, p, a1s.at[0], sem, **to(core_peer)).wait_recv()

        def sent(self, c, copies):
            def body(k):
                for cp in copies(c, k):
                    cp.wait_send()

            loop(3, body)

        def a3_wait(self, c):
            self.sent(c, self.a3_copies)

        def a2_wait(self, c):
            self.sent(c, self.a2_copies)

        def a1_wait(self, c):
            self.sent(c, self.a1_copies)

        def a3(self, c):
            pl.when(c > 0)(lambda: big.a3_wait(c - 1))

            def body(k):
                b1, b2, b3 = bits(k)
                self.landed(g3.at[lax.rem(c, 2), k], self.place(c, k, b1, b2, 1 - b3))
                for cp in self.a3_copies(c, k):
                    cp.start()

            loop(3, body)

        def a2(self, c):
            pl.when(c > 0)(lambda: big.a2_wait(c - 1))

            def body(k):
                b1, b2, b3 = bits(k)
                self.landed(g2.at[lax.rem(c, 2), k, 0], self.place(c, k, b1, 1 - b2, b3))
                self.landed(g2.at[lax.rem(c, 2), k, 1], self.place(c, k, b1, 1 - b2, 1 - b3))
                self.f_copies(c, k)[3].wait()
                for cp in self.a2_copies(c, k):
                    cp.start()

            loop(3, body)

        def a1(self, c):
            pl.when(c > 0)(lambda: big.a1_wait(c - 1))

            def body(k):
                b1, b2, b3 = bits(k)
                for i, part in enumerate((b3, 1 - b3)):
                    self.landed(g1.at[lax.rem(c, 2), k, i], self.place(c, k, 1 - b1, b2, part))
                self.landed(g1.at[lax.rem(c, 2), k, 2], self.part_of_y(c, col(k, b0, 1 - b1, 1 - b2), CB))
                for cp in self.a1_copies(c, k):
                    cp.start()

            loop(3, body)

        def a0_wait(self, c):
            def body(k):
                b1, _, _ = bits(k)
                for i, i1 in enumerate((b1, 1 - b1)):
                    self.landed(g0.at[c, k, i], self.part_of_y(c, col(k, 1 - b0, i1, 0), 2 * CB))

            loop(3, body)

        def early(self, c):
            self.gu_epilogue(c, nt - 1)

            @pl.when(c > 0)
            def _():
                for i in range(4):
                    pl.semaphore_wait(credit.at[i], 1)

            self.s0(c, True)
            self.s1(c)
            either(c + 1, lambda a: a.x_copy(c + 1, 1).start(priority=1))
            self.s0(c, False)

    big, small = Chunk(BIG), Chunk(rows - nb * BIG)

    def either(c, act):
        pl.when((c >= 0) & (c < nb))(lambda: act(big))
        pl.when(c == nb)(lambda: act(small))

    for i in range(PACKETS):
        for cp in w_copies(i):
            cp.start()
        big.x_copy(0, i).start()

    barrier = pltpu.get_barrier_semaphore()
    everyone = [peer(0), peer(1), peer(2), core_peer]
    for dev in everyone:
        pl.semaphore_signal(barrier, inc=1, **to(dev))
    pl.semaphore_wait(barrier, 4)

    def chunk(c):
        def tile(n):
            for i in range(PACKETS):
                either(c, lambda a: a.gate_up(c, n, i))
                if i == 0:
                    @pl.when((c == 0) & (n == 1))
                    def _():
                        for j in range(3):
                            d_copy(j).start()

                for slot, act, lag in SLOTS:
                    if slot % PACKETS == i:
                        pl.when(n == slot // PACKETS)(
                            lambda act=act, lag=lag: either(c - lag, lambda a: getattr(a, act)(c - lag)))

        loop(nt, tile)
        either(c, lambda a: a.early(c))

    loop(nc + 2, chunk)

    last = nc - 1
    def drain(k):
        for j in range(2):
            small.s0_copy(k, False, j).wait_send()
        for j in range(2):
            small.s1_copy(k, j).wait_send()
        for j in range(2):
            small.s2_copy(k, j).wait_send()
        small.s3_copy(k).wait_send()

    loop(3, drain)
    small.f_wait(last)
    small.a3_wait(last)
    small.a2_wait(last)
    small.a1_wait(last)
    loop(nc, lambda c: either(c, lambda a: a.a0_wait(c)))


def block(x, wg, wu, wd):
    rows, depth = x.shape
    units = wg.shape[1]
    nc = rows // BIG + 1
    kb = depth // PACKETS
    dma, vmem = pltpu.SemaphoreType.DMA, pltpu.VMEM
    y = pl.pallas_call(
        kernel,
        name="mlp",
        out_shape=jax.ShapeDtypeStruct((rows, depth), BF16),
        in_specs=[pl.BlockSpec(memory_space=pl.ANY)] * 4,
        out_specs=pl.BlockSpec(memory_space=pl.ANY),
        scratch_shapes=[
            vmem((PACKETS, BIG, kb), BF16),
            vmem((W_SLOTS, kb, 2 * GN), BF16),
            vmem((BIG, 2 * GN), F32),
            vmem((2, BIG, units), BF16),
            vmem((3, units, 2 * CB), BF16),
            vmem((3, BIG, CB), F32),
            vmem((3, 4, BIG, CB), BF16),
            vmem((3, 2, BIG, CB), BF16),
            vmem((3, BIG, CB), BF16),
            vmem((3, BIG // 2, CB), BF16),
            vmem((15, BIG, CB), BF16),
            vmem((3, BIG // 2, CB), BF16),
            vmem((3, BIG // 2, CB), BF16),
            dma((PACKETS,)), dma((W_SLOTS, 2)), dma((3,)),
            dma((6,)), dma((3, 2)), dma((3, 2)), dma((3,)), dma((3, 3)), dma((3,)),
            dma((3, 2)), dma((3, 2)), dma((3,)),
            dma((3, 4)), dma((3, 2)), dma((3, 2)), dma((3,)),
            dma((2, 3)), dma((2, 3, 2)), dma((2, 3, 3)), dma((nc, 3, 2)),
            pltpu.SemaphoreType.REGULAR((4,)),
        ],
        compiler_params=pltpu.CompilerParams(
            collective_id=0, has_side_effects=True, vmem_limit_bytes=67_043_328
        ),
    )(x, wg, wu, wd)

    def put(a, b):
        b[...] = a[...]

    return pl.pallas_call(
        put,
        name="put",
        grid=(rows // 256,),
        out_shape=jax.ShapeDtypeStruct((rows, depth), BF16),
        in_specs=[pl.BlockSpec((256, depth), lambda i: (i, 0))],
        out_specs=pl.BlockSpec((256, depth), lambda i: (i, 0)),
        compiler_params=pltpu.CompilerParams(vmem_limit_bytes=40 * 2**20),
    )(y)


def solution(mesh):
    return jax.shard_map(
        block,
        mesh=mesh,
        in_specs=(P("dp", None), P(None, "tp"), P(None, "tp"), P("tp", None)),
        out_specs=P("dp", None),
        check_vma=False,
    )
```

time: 432 us -> 414 us (0.958)
  local copies, waits for them, and re-layouts: 33.7 us -> 0 us
  Pallas kernels: 398 us -> 414 us
    unnamed x1 -> x0, local copies, waits for them, and re-layouts: 33.7 us -> none
    pallas_call x0 -> x1, Pallas kernels: none -> 32.3 us  [block(): pl.pallas_call(put, name='put', grid=(rows // 256,), out_shape=jax.ShapeD...]
    pallas_call x1, Pallas kernels: 398 us -> 382 us  [block(): pl.pallas_call(kernel, name='mlp', out_shape=jax.ShapeDtypeStruct((rows,...]
where the time goes in v3:
time: 414 us
  Pallas kernels  414 us (100%)
    pallas_call x1, Pallas kernels, block(): pl.pallas_call(kernel, name='mlp', out_shape=jax.ShapeDtypeStruct((rows,...  382 us
    pallas_call x1, Pallas kernels, block(): pl.pallas_call(put, name='put', grid=(rows // 256,), out_shape=jax.ShapeD...  32.3 us

profile of v3, /device:TPU:0, one launch (start us, length us, event | category | flops | bytes accessed | tf_op | source)
XLA Modules:
  0.0 414.0 jit_solution(15959658977909610189)
XLA Ops:
  0.0 381.7 %mlp.1.a = bf16[2048,12288]{1,0:T(8,128)(2,1)} custom-call(bf16[2048,12288]{1,0:T(8,128)(2,1)} %x_hbm.1, bf16[12288,1792]{1,0:T(8,128)(2,1)} %wg_hbm.1, bf16[12288,1792]{1,0:T(8,128)(2,1)} %wu_hbm.1, bf16[1792,12288]{1,0:T(8,128)(2,1)} %wd_hbm.1), custom_call_target="tpu_custom_call" | custom-call | tf_op jit(solution)/shard_map/mlp/pallas_call | solution.py:457
  381.7 32.3 %put.1 = bf16[2048,12288]{1,0:T(8,128)(2,1)} custom-call(bf16[2048,12288]{1,0:T(8,128)(2,1)} %mlp.1.a), custom_call_target="tpu_custom_call" | custom-call | tf_op jit(solution)/shard_map/put/pallas_call | solution.py:492

commit v4 on v3

--- a/solution.py
+++ b/solution.py
@@ -13,15 +13,36 @@
 PACKETS = 2
 W_SLOTS = 3
 GN = 256
+STRIP = 32
+STRIPS, AHEAD = 8, 6
 D_STEPS = 12
 
 SLOTS = ((1, "s2", 1), (4, "s3", 1), (5, "a2", 2), (8, "fin", 1), (12, "a1", 2), (12, "a3", 1))
 
 
-def kernel(x_hbm, wg_hbm, wu_hbm, wd_hbm, y_hbm,
-           xv, wbuf, acc, hv, dbuf, raw, rv0, rv1, rv2, rv3, st, st3, stf,
+def kept(depth):
+    return W_SLOTS * (depth // PACKETS) * 2 * GN // depth, BIG
+
+
+def kept_parts(depth, y, wbuf, xv):
+    in_w, in_x = kept(depth)
+    kb = depth // PACKETS
+    per = kb // in_w
+
+    def w_part(i):
+        part = pl.ds(pl.multiple_of(lax.rem(i, per) * in_w, 16), in_w)
+        return y.at[pl.ds(0, in_w), pl.ds(pl.multiple_of(i * CB, CB), CB)], wbuf.at[i // per, part]
+
+    def x_part(i):
+        return y.at[pl.ds(in_w, in_x), pl.ds(pl.multiple_of(i * kb, kb), kb)], xv.at[i]
+
+    return [(depth // CB, w_part), (PACKETS, x_part)]
+
+
+def kernel(x_hbm, wg_hbm, wu_hbm, wd_hbm, y_hbm, wbuf, xv,
+           acc, hv, dbuf, raw, rv0, rv1, rv2, rv3, st,
            x_sem, w_sem, d_sem, s0s, s1s, s2s, s3s, fs, fl, a3s, a2s, a1s,
-           r0, r1, r2, r3, g3, g2, g1, g0, credit):
+           r0, r1, r2, r3, g3, g2, g1, g0, k_sem, credit):
     rows, depth = x_hbm.shape
     units = wg_hbm.shape[1]
     kb = depth // PACKETS
@@ -155,14 +176,15 @@
 
         def s0(self, c, first):
             def ready(k):
-                def wait(chunk):
+                if first:
+                    @pl.when(c > 0)
+                    def _():
+                        for j in range(2):
+                            big.s2_copy(k, j).wait_send()
+                        big.s0_copy(k, first, 1).wait_send()
+                else:
                     for j in range(2):
-                        chunk.s0_copy(k, first, j).wait_send()
-
-                if first:
-                    pl.when(c > 0)(lambda: wait(big))
-                else:
-                    wait(self)
+                        self.s0_copy(k, first, j).wait_send()
 
             self.pairs(c, c * D_STEPS + (0 if first else 6), ready, lambda k, i2: [], lambda k, j: k * 2 + j,
                        lambda k, j: self.s0_copy(k, first, j).start())
@@ -187,7 +209,11 @@
             def ready(k):
                 for j in range(2):
                     self.r0_wait(k, index(k, j))
-                    pl.when(c > 0)(lambda j=j: big.s1_copy(k, j).wait_send())
+
+                @pl.when(c > 0)
+                def _():
+                    big.f_wait(c - 1, k, True)
+                    big.s1_copy(k, 1).wait_send()
 
             self.pairs(c, c * D_STEPS + 3, ready, lambda k, i2: [rv0.at[k, (1 - bits(k)[0]) * 2 + i2]],
                        lambda k, j: 6 + k * 2 + j, lambda k, j: self.s1_copy(k, j).start())
@@ -196,7 +222,7 @@
             b3 = bits(k)[2]
             part = pl.ds(pl.multiple_of((1 - b3 if i == 0 else b3) * self.half, 16), self.half)
             return pltpu.make_async_remote_copy(
-                st.at[12 + k, part], rv2.at[k, part], s2s.at[k, i], r2.at[k, i], **to(peer(dim(k, 1))))
+                st.at[k * 2, part], rv2.at[k, part], s2s.at[k, i], r2.at[k, i], **to(peer(dim(k, 1))))
 
         def s2(self, c):
             def body(k):
@@ -206,12 +232,11 @@
                 d_copy(step).wait()
                 self.r0_wait(k, i)
                 self.r1_wait(k, 1 - b2)
-                for j in range(2):
-                    pl.when(c > 0)(lambda j=j: big.s2_copy(k, j).wait_send())
+                self.s0_copy(k, False, 0).wait_send()
                 y = self.down(c, k, 1 - b2)
                 for a in (rv0.at[k, i], rv1.at[k, 1 - b2]):
                     y = y + a[pl.ds(0, self.R)].astype(F32)
-                st[12 + k, pl.ds(0, self.R)] = y.astype(BF16)
+                st[k * 2, pl.ds(0, self.R)] = y.astype(BF16)
                 raw[k, pl.ds(0, self.R)] = self.down(c, k, b2)
                 for i in range(2):
                     self.s2_copy(k, i).start()
@@ -219,7 +244,7 @@
 
             loop(3, body)
 
-        def last(self, k, part, more, dst):
+        def last(self, k, part, more):
             b1, b2, _ = bits(k)
             rows = pl.ds(pl.multiple_of(part * self.half, 16), self.half)
             y = raw[k, rows]
@@ -227,12 +252,12 @@
                 y = y + a[rows].astype(F32)
             if more:
                 y = y + rv3[k, pl.ds(0, self.half)].astype(F32)
-            dst[k, pl.ds(0, self.half)] = y.astype(BF16)
+            st[6 + k * 2, pl.ds(0, self.half)] = y.astype(BF16)
 
         def s3_copy(self, k):
             n = pl.ds(0, self.half)
             return pltpu.make_async_remote_copy(
-                st3.at[k, n], rv3.at[k, n], s3s.at[k], r3.at[k], **to(peer(dim(k, 2))))
+                st.at[6 + k * 2, n], rv3.at[k, n], s3s.at[k], r3.at[k], **to(peer(dim(k, 2))))
 
         def s3(self, c):
             def body(k):
@@ -240,8 +265,8 @@
                 self.r0_wait(k, b1 * 2 + b2)
                 self.r1_wait(k, b2)
                 self.s2_copy(k, 0).wait_recv()
-                pl.when(c > 0)(lambda: big.s3_copy(k).wait_send())
-                self.last(k, 1 - b3, False, st3)
+                self.s1_copy(k, 0).wait_send()
+                self.last(k, 1 - b3, False)
                 self.s3_copy(k).start()
 
             loop(3, body)
@@ -253,7 +278,7 @@
         def f_copies(self, c, k):
             b1, b2, b3 = bits(k)
             par = lax.rem(c, 2)
-            src, dst = stf.at[k, pl.ds(0, self.half)], self.place(c, k, b1, b2, b3)
+            src, dst = st.at[6 + k * 2, pl.ds(0, self.half)], self.place(c, k, b1, b2, b3)
             return [
                 pltpu.make_async_remote_copy(src, dst, fs.at[k, 0], g3.at[par, k], **to(peer(dim(k, 2)))),
                 pltpu.make_async_remote_copy(src, dst, fs.at[k, 1], g2.at[par, k, 0], **to(peer(dim(k, 1)))),
@@ -261,22 +286,19 @@
                 pltpu.make_async_copy(src, dst, fl.at[k]),
             ]
 
-        def f_wait(self, c):
-            def body(k):
-                copies = self.f_copies(c, k)
-                for cp in copies[:3]:
-                    cp.wait_send()
-
-            loop(3, body)
+        def f_wait(self, c, k, copies):
+            for cp in self.f_copies(c, k)[:3]:
+                cp.wait_send()
+            if copies:
+                self.f_copies(c, k)[3].wait()
 
         def fin(self, c):
-            pl.when(c > 0)(lambda: big.f_wait(c - 1))
-
             def body(k):
                 _, _, b3 = bits(k)
                 self.s2_copy(k, 1).wait_recv()
                 self.s3_copy(k).wait_recv()
-                self.last(k, b3, True, stf)
+                self.s3_copy(k).wait_send()
+                self.last(k, b3, True)
                 copies = self.f_copies(c, k)
                 copies[0].start()
                 copies[3].start()
@@ -353,7 +375,8 @@
                 b1, b2, b3 = bits(k)
                 self.landed(g2.at[lax.rem(c, 2), k, 0], self.place(c, k, b1, 1 - b2, b3))
                 self.landed(g2.at[lax.rem(c, 2), k, 1], self.place(c, k, b1, 1 - b2, 1 - b3))
-                self.f_copies(c, k)[3].wait()
+                if self is small:
+                    self.f_copies(c, k)[3].wait()
                 for cp in self.a2_copies(c, k):
                     cp.start()
 
@@ -410,8 +433,21 @@
         pl.semaphore_signal(barrier, inc=1, **to(dev))
     pl.semaphore_wait(barrier, 4)
 
+    rooms = kept_parts(depth, y_hbm, wbuf, xv)
+
+    def keep(act):
+        base = 0
+        for count, part in rooms:
+            loop(count, lambda i, base=base, part=part: act(pltpu.make_async_copy(*part(i), k_sem.at[base + i])))
+            base += count
+
     def chunk(c):
         def tile(n):
+            @pl.when((c == nc) & (n == 1))
+            def _():
+                loop(nc - 2, lambda i: big.a0_wait(i))
+                keep(lambda cp: cp.start())
+
             for i in range(PACKETS):
                 either(c, lambda a: a.gate_up(c, n, i))
                 if i == 0:
@@ -432,20 +468,19 @@
 
     last = nc - 1
     def drain(k):
-        for j in range(2):
-            small.s0_copy(k, False, j).wait_send()
-        for j in range(2):
-            small.s1_copy(k, j).wait_send()
+        small.s0_copy(k, False, 1).wait_send()
+        small.s1_copy(k, 1).wait_send()
         for j in range(2):
             small.s2_copy(k, j).wait_send()
-        small.s3_copy(k).wait_send()
+        small.f_wait(last, k, False)
 
     loop(3, drain)
-    small.f_wait(last)
     small.a3_wait(last)
     small.a2_wait(last)
     small.a1_wait(last)
-    loop(nc, lambda c: either(c, lambda a: a.a0_wait(c)))
+    big.a0_wait(nc - 2)
+    small.a0_wait(nc - 1)
+    keep(lambda cp: cp.wait())
 
 
 def block(x, wg, wu, wd):
@@ -454,15 +489,17 @@
     nc = rows // BIG + 1
     kb = depth // PACKETS
     dma, vmem = pltpu.SemaphoreType.DMA, pltpu.VMEM
-    y = pl.pallas_call(
+    y, wbuf, xv = pl.pallas_call(
         kernel,
         name="mlp",
-        out_shape=jax.ShapeDtypeStruct((rows, depth), BF16),
+        out_shape=[
+            jax.ShapeDtypeStruct((rows, depth), BF16),
+            vmem((W_SLOTS, kb, 2 * GN), BF16),
+            vmem((PACKETS, BIG, kb), BF16),
+        ],
         in_specs=[pl.BlockSpec(memory_space=pl.ANY)] * 4,
-        out_specs=pl.BlockSpec(memory_space=pl.ANY),
+        out_specs=[pl.BlockSpec(memory_space=pl.ANY)] + [pl.BlockSpec(memory_space=pltpu.VMEM)] * 2,
         scratch_shapes=[
-            vmem((PACKETS, BIG, kb), BF16),
-            vmem((W_SLOTS, kb, 2 * GN), BF16),
             vmem((BIG, 2 * GN), F32),
             vmem((2, BIG, units), BF16),
             vmem((3, units, 2 * CB), BF16),
@@ -471,33 +508,76 @@
             vmem((3, 2, BIG, CB), BF16),
             vmem((3, BIG, CB), BF16),
             vmem((3, BIG // 2, CB), BF16),
-            vmem((15, BIG, CB), BF16),
-            vmem((3, BIG // 2, CB), BF16),
-            vmem((3, BIG // 2, CB), BF16),
+            vmem((12, BIG, CB), BF16),
             dma((PACKETS,)), dma((W_SLOTS, 2)), dma((3,)),
             dma((6,)), dma((3, 2)), dma((3, 2)), dma((3,)), dma((3, 3)), dma((3,)),
             dma((3, 2)), dma((3, 2)), dma((3,)),
             dma((3, 4)), dma((3, 2)), dma((3, 2)), dma((3,)),
             dma((2, 3)), dma((2, 3, 2)), dma((2, 3, 3)), dma((nc, 3, 2)),
+            dma((depth // CB + PACKETS,)),
             pltpu.SemaphoreType.REGULAR((4,)),
         ],
         compiler_params=pltpu.CompilerParams(
-            collective_id=0, has_side_effects=True, vmem_limit_bytes=67_043_328
+            collective_id=0, has_side_effects=True, vmem_limit_bytes=75 * 2**19
         ),
     )(x, wg, wu, wd)
-
-    def put(a, b):
-        b[...] = a[...]
 
     return pl.pallas_call(
         put,
         name="put",
-        grid=(rows // 256,),
         out_shape=jax.ShapeDtypeStruct((rows, depth), BF16),
-        in_specs=[pl.BlockSpec((256, depth), lambda i: (i, 0))],
-        out_specs=pl.BlockSpec((256, depth), lambda i: (i, 0)),
-        compiler_params=pltpu.CompilerParams(vmem_limit_bytes=40 * 2**20),
-    )(y)
+        in_specs=[pl.BlockSpec(memory_space=pl.ANY)] + [pl.BlockSpec(memory_space=pltpu.VMEM)] * 2,
+        out_specs=pl.BlockSpec(memory_space=pl.ANY),
+        scratch_shapes=[
+            vmem((STRIPS, STRIP, depth), BF16),
+            dma((depth // CB + PACKETS,)),
+            dma((STRIPS, 2)),
+        ],
+        compiler_params=pltpu.CompilerParams(vmem_limit_bytes=7 * 2**20),
+    )(y, wbuf, xv)
+
+
+def put(y_hbm, wbuf, xv, o_hbm, buf, k_sem, sem):
+    rows, depth = o_hbm.shape
+    first = sum(kept(depth))
+    count = (rows - first) // STRIP
+
+    def strip(i):
+        part, slot = pl.ds(pl.multiple_of(first + i * STRIP, STRIP), STRIP), lax.rem(i, STRIPS)
+        return (pltpu.make_async_copy(y_hbm.at[part], buf.at[slot], sem.at[slot, 0]),
+                pltpu.make_async_copy(buf.at[slot], o_hbm.at[part], sem.at[slot, 1]))
+
+    def keep(act):
+        base = 0
+        for n, part in kept_parts(depth, o_hbm, wbuf, xv):
+            def one(i, _, base=base, part=part):
+                dst, src = part(i)
+                act(pltpu.make_async_copy(src, dst, k_sem.at[base + i]))
+                return 0
+
+            lax.fori_loop(0, n, one, 0)
+            base += n
+
+    for i in range(AHEAD):
+        strip(i)[0].start()
+    keep(lambda cp: cp.start())
+
+    def step(i, _):
+        strip(i)[0].wait()
+        strip(i)[1].start()
+        j = i + AHEAD
+
+        @pl.when(j < count)
+        def _():
+            pl.when(j >= STRIPS)(lambda: strip(j - STRIPS)[1].wait())
+            strip(j)[0].start()
+
+        return 0
+
+    lax.fori_loop(0, count, step, 0)
+    keep(lambda cp: cp.wait())
+    for i in range(count - STRIPS, count):
+        strip(i)[1].wait()
 
 
 def solution(mesh):

time: 414 us -> 407 us (0.983)
  Pallas kernels: 414 us -> 407 us
    pallas_call x2, Pallas kernels: 414 us -> 407 us  [the longest x1 382 us: block(): pl.pallas_call(kernel, name='mlp', out_shape=[jax.ShapeDtypeStruct((rows,...]
where the time goes in v4:
time: 407 us
  Pallas kernels  407 us (100%)
    pallas_call x1, Pallas kernels, block(): pl.pallas_call(kernel, name='mlp', out_shape=[jax.ShapeDtypeStruct((rows,...  382 us
    pallas_call x1, Pallas kernels, block(): pl.pallas_call(put, name='put', out_shape=jax.ShapeDtypeStruct((rows, dep...  24.8 us

profile of v4, /device:TPU:0, one launch (start us, length us, event | category | flops | bytes accessed | tf_op | source)
XLA Modules:
  0.0 407.0 jit_solution(1063282736272270386)
XLA Ops:
  0.0 382.2 %mlp.1 = (bf16[2048,12288]{1,0:T(8,128)(2,1)}, bf16[3,6144,512]{2,1,0:T(8,128)(2,1)S(1)}, bf16[2,352,6144]{2,1,0:T(8,128)(2,1)S(1)}) custom-call(bf16[2048,12288]{1,0:T(8,128)(2,1)} %x_hbm.1, bf16[12288,1792]{1,0:T(8,128)(2,1)} %wg_hbm.1, bf16[12288,1792]{1,0:T(8,128)(2,1)} %wu_hbm.1, bf16[1792,12288]{1,0:T(8,128)(2,1)} %wd_hbm.1), custom_call_target="tpu_custom_call" | custom-call | tf_op jit(solution)/shard_map/mlp/pallas_call | solution.py:492
  382.2 24.8 %put.1 = bf16[2048,12288]{1,0:T(8,128)(2,1)} custom-call(bf16[2048,12288]{1,0:T(8,128)(2,1)} %get-tuple-element.8.y_hbm, bf16[3,6144,512]{2,1,0:T(8,128)(2,1)S(1)} %get-tuple-element.9.wbuf, bf16[2,352,6144]{2,1,0:T(8,128)(2,1)S(1)} %get-tuple-element.10.xv), custom_call_target="tpu_custom_call" | custom-call | tf_op jit(solution)/shard_map/put/pallas_call | solution.py:525

commit v5 on v4

--- a/solution.py
+++ b/solution.py
@@ -53,6 +53,8 @@
     b0 = lax.rem(me, 2)
 
     def mask(d):
+        if isinstance(d, int):
+            return (8, 4, 2)[d]
         return jnp.where(d == 0, 8, jnp.where(d == 1, 4, 2))
 
     def bit(d):
@@ -65,7 +67,7 @@
     core_peer = me + 1 - 2 * b0
 
     def dim(k, s):
-        return lax.rem(k + s, 3)
+        return (k + s) % 3 if isinstance(k, int) else lax.rem(k + s, 3)
 
     def bits(k):
         return bit(dim(k, 0)), bit(dim(k, 1)), bit(dim(k, 2))
@@ -83,24 +85,24 @@
 
         lax.fori_loop(0, n, step, 0)
 
-    def w_copies(q):
-        n, kk, slot = lax.rem(q // PACKETS, nt), lax.rem(q, PACKETS), lax.rem(q, W_SLOTS)
-        src = (pl.ds(pl.multiple_of(kk * kb, kb), kb), pl.ds(pl.multiple_of(n * GN, GN), GN))
+    def w_copies(n, kk, slot):
+        src = (pl.ds(kk * kb, kb), pl.ds(pl.multiple_of(n * GN, GN), GN))
         return [
             pltpu.make_async_copy(wg_hbm.at[src], wbuf.at[slot, :, pl.ds(0, GN)], w_sem.at[slot, 0]),
             pltpu.make_async_copy(wu_hbm.at[src], wbuf.at[slot, :, pl.ds(GN, GN)], w_sem.at[slot, 1]),
         ]
 
-    def w_next(q):
-        for cp in w_copies(q):
+    def w_next(c, n, kk):
+        slot = lax.rem((c * nt + n) * PACKETS + kk, W_SLOTS)
+        for cp in w_copies(n, kk, slot):
             cp.wait()
 
-        @pl.when(q + W_SLOTS - 1 < nc * nt * PACKETS)
+        @pl.when((c < nc - 1) | (n < nt - 1))
         def _():
-            for cp in w_copies(q + W_SLOTS - 1):
+            for cp in w_copies(jnp.where(n == nt - 1, 0, n + 1), kk, jnp.where(slot == 0, W_SLOTS - 1, slot - 1)):
                 cp.start(priority=1)
 
-        return lax.rem(q, W_SLOTS)
+        return slot
 
     def d_copy(step):
         r, slot = lax.rem(step, D_STEPS), lax.rem(step, 3)
@@ -130,7 +132,7 @@
 
         def gate_up(self, c, n, i):
             pl.when(n == 0)(lambda: self.x_copy(c, i).wait())
-            slot = w_next((c * nt + n) * PACKETS + i)
+            slot = w_next(c, n, i)
             if i == 0:
                 self.gu_epilogue(c, lax.rem(n + nt - 1, nt))
             d = jnp.dot(xv[i, pl.ds(0, self.R)], wbuf[slot], preferred_element_type=F32)
@@ -158,7 +160,8 @@
                     send(k, j)
                 d_start(step0 + k + 3)
 
-            loop(3, pair)
+            for k in range(3):
+                pair(k)
 
         def whole(self, ref):
             return ref.at[pl.ds(0, self.R)]
@@ -242,7 +245,8 @@
                     self.s2_copy(k, i).start()
                 d_start(step + 3)
 
-            loop(3, body)
+            for k in range(3):
+                body(k)
 
         def last(self, k, part, more):
             b1, b2, _ = bits(k)
@@ -325,21 +329,28 @@
             ]
 
         def a2_copies(self, c, k):
-            b1, b2, _ = bits(k)
-            p = self.part_of_y(c, col(k, b0, b1, 1 - b2), CB)
+            b1, b2, b3 = bits(k)
+            par = lax.rem(c, 2)
+            block = self.part_of_y(c, col(k, b0, b1, 1 - b2), CB)
+            pieces = [self.place(c, k, b1, 1 - b2, b3), self.place(c, k, b1, 1 - b2, 1 - b3)]
             q = self.part_of_y(c, col(k, b0, b1, 0), 2 * CB)
             return [
-                pltpu.make_async_remote_copy(p, p, a2s.at[k, 0], g1.at[lax.rem(c, 2), k, 2], **to(peer(dim(k, 0)))),
-                pltpu.make_async_remote_copy(q, q, a2s.at[k, 1], g0.at[c, k, 0], **to(core_peer)),
-            ]
+                pltpu.make_async_remote_copy(p, p, a2s.at[k, i], g1.at[par, k, 2 + i], **to(peer(dim(k, 0))))
+                for i, p in enumerate(pieces if self is small else [block])
+            ] + [pltpu.make_async_remote_copy(q, q, a2s.at[k, 2], g0.at[c, k, 0], **to(core_peer))]
+
+        def a1_parts(self, c, k):
+            b1, b2, _ = bits(k)
+            if self is small:
+                return [self.part_of_y(c, col(k, b0, 1 - b1, i2), CB) for i2 in (b2, 1 - b2)]
+            return [self.part_of_y(c, col(k, b0, 1 - b1, 0), 2 * CB)]
 
         def a1_copies(self, c, k):
-            b1, _, _ = bits(k)
-            q = self.part_of_y(c, col(k, b0, 1 - b1, 0), 2 * CB)
-            return [pltpu.make_async_remote_copy(q, q, a1s.at[k], g0.at[c, k, 1], **to(core_peer))]
+            return [pltpu.make_async_remote_copy(q, q, a1s.at[k, i], g0.at[c, k, 1 + i], **to(core_peer))
+                    for i, q in enumerate(self.a1_parts(c, k))]
 
         def landed(self, sem, p):
-            pltpu.make_async_remote_copy(p, p, a1s.at[0], sem, **to(core_peer)).wait_recv()
+            pltpu.make_async_remote_copy(p, p, a1s.at[0, 0], sem, **to(core_peer)).wait_recv()
 
         def sent(self, c, copies):
             def body(k):
@@ -371,35 +382,66 @@
         def a2(self, c):
             pl.when(c > 0)(lambda: big.a2_wait(c - 1))
 
-            def body(k):
+            def piece(k, i):
                 b1, b2, b3 = bits(k)
-                self.landed(g2.at[lax.rem(c, 2), k, 0], self.place(c, k, b1, 1 - b2, b3))
-                self.landed(g2.at[lax.rem(c, 2), k, 1], self.place(c, k, b1, 1 - b2, 1 - b3))
-                if self is small:
-                    self.f_copies(c, k)[3].wait()
-                for cp in self.a2_copies(c, k):
+                self.landed(g2.at[lax.rem(c, 2), k, i], self.place(c, k, b1, 1 - b2, b3 if i == 0 else 1 - b3))
+
+            def first(k):
+                self.f_copies(c, k)[3].wait()
+                piece(k, 0)
+                self.a2_copies(c, k)[0].start()
+
+            def body(k):
+                if self is not small:
+                    piece(k, 0)
+                piece(k, 1)
+                for cp in self.a2_copies(c, k)[1 if self is small else 0 :]:
                     cp.start()
 
+            if self is small:
+                loop(3, first)
             loop(3, body)
 
         def a1(self, c):
             pl.when(c > 0)(lambda: big.a1_wait(c - 1))
 
-            def body(k):
+            def near(k):
                 b1, b2, b3 = bits(k)
                 for i, part in enumerate((b3, 1 - b3)):
                     self.landed(g1.at[lax.rem(c, 2), k, i], self.place(c, k, 1 - b1, b2, part))
-                self.landed(g1.at[lax.rem(c, 2), k, 2], self.part_of_y(c, col(k, b0, 1 - b1, 1 - b2), CB))
-                for cp in self.a1_copies(c, k):
-                    cp.start()
-
+
+            def far(k):
+                b1, b2, b3 = bits(k)
+                if self is small:
+                    for i, part in enumerate((b3, 1 - b3)):
+                        self.landed(g1.at[lax.rem(c, 2), k, 2 + i], self.place(c, k, 1 - b1, 1 - b2, part))
+                else:
+                    self.landed(g1.at[lax.rem(c, 2), k, 2], self.part_of_y(c, col(k, b0, 1 - b1, 1 - b2), CB))
+
+            def first(k):
+                near(k)
+                self.a1_copies(c, k)[0].start()
+
+            def body(k):
+                if self is not small:
+                    near(k)
+                far(k)
+                self.a1_copies(c, k)[-1].start()
+
+            if self is small:
+                loop(3, first)
             loop(3, body)
 
         def a0_wait(self, c):
             def body(k):
                 b1, _, _ = bits(k)
-                for i, i1 in enumerate((b1, 1 - b1)):
-                    self.landed(g0.at[c, k, i], self.part_of_y(c, col(k, 1 - b0, i1, 0), 2 * CB))
+                self.landed(g0.at[c, k, 0], self.part_of_y(c, col(k, 1 - b0, b1, 0), 2 * CB))
+                if self is small:
+                    _, b2, _ = bits(k)
+                    for i, i2 in enumerate((b2, 1 - b2)):
+                        self.landed(g0.at[c, k, 1 + i], self.part_of_y(c, col(k, 1 - b0, 1 - b1, i2), CB))
+                else:
+                    self.landed(g0.at[c, k, 1], self.part_of_y(c, col(k, 1 - b0, 1 - b1, 0), 2 * CB))
 
             loop(3, body)
 
@@ -423,7 +465,7 @@
         pl.when(c == nb)(lambda: act(small))
 
     for i in range(PACKETS):
-        for cp in w_copies(i):
+        for cp in w_copies(0, i, i):
             cp.start()
         big.x_copy(0, i).start()
 
@@ -451,10 +493,7 @@
             for i in range(PACKETS):
                 either(c, lambda a: a.gate_up(c, n, i))
                 if i == 0:
-                    @pl.when((c == 0) & (n == 1))
-                    def _():
-                        for j in range(3):
-                            d_copy(j).start()
+                    pl.when((c == 0) & (n >= 3) & (n < 6))(lambda: d_copy(n - 3).start())
 
                 for slot, act, lag in SLOTS:
                     if slot % PACKETS == i:
@@ -511,9 +550,9 @@
             vmem((12, BIG, CB), BF16),
             dma((PACKETS,)), dma((W_SLOTS, 2)), dma((3,)),
             dma((6,)), dma((3, 2)), dma((3, 2)), dma((3,)), dma((3, 3)), dma((3,)),
-            dma((3, 2)), dma((3, 2)), dma((3,)),
+            dma((3, 2)), dma((3, 3)), dma((3, 2)),
             dma((3, 4)), dma((3, 2)), dma((3, 2)), dma((3,)),
-            dma((2, 3)), dma((2, 3, 2)), dma((2, 3, 3)), dma((nc, 3, 2)),
+            dma((2, 3)), dma((2, 3, 2)), dma((2, 3, 4)), dma((nc, 3, 3)),
             dma((depth // CB + PACKETS,)),
             pltpu.SemaphoreType.REGULAR((4,)),
         ],

time: 407 us -> 404 us (level)
  no operation moved by 1% of the time
where the time goes in v5:
time: 404 us
  Pallas kernels  404 us (100%)
    pallas_call x1, Pallas kernels, block(): pl.pallas_call(kernel, name='mlp', out_shape=[jax.ShapeDtypeStruct((rows,...  380 us
    pallas_call x1, Pallas kernels, block(): pl.pallas_call(put, name='put', out_shape=jax.ShapeDtypeStruct((rows, dep...  24.8 us

profile of v5, /device:TPU:0, one launch (start us, length us, event | category | flops | bytes accessed | tf_op | source)
XLA Modules:
  0.0 404.3 jit_solution(7257451638514911724)
XLA Ops:
  0.0 379.6 %mlp.1 = (bf16[2048,12288]{1,0:T(8,128)(2,1)}, bf16[3,6144,512]{2,1,0:T(8,128)(2,1)S(1)}, bf16[2,352,6144]{2,1,0:T(8,128)(2,1)S(1)}) custom-call(bf16[2048,12288]{1,0:T(8,128)(2,1)} %x_hbm.1, bf16[12288,1792]{1,0:T(8,128)(2,1)} %wg_hbm.1, bf16[12288,1792]{1,0:T(8,128)(2,1)} %wu_hbm.1, bf16[1792,12288]{1,0:T(8,128)(2,1)} %wd_hbm.1), custom_call_target="tpu_custom_call" | custom-call | tf_op jit(solution)/shard_map/mlp/pallas_call | solution.py:531
  379.6 24.8 %put.1 = bf16[2048,12288]{1,0:T(8,128)(2,1)} custom-call(bf16[2048,12288]{1,0:T(8,128)(2,1)} %get-tuple-element.8.y_hbm, bf16[3,6144,512]{2,1,0:T(8,128)(2,1)S(1)} %get-tuple-element.9.wbuf, bf16[2,352,6144]{2,1,0:T(8,128)(2,1)S(1)} %get-tuple-element.10.xv), custom_call_target="tpu_custom_call" | custom-call | tf_op jit(solution)/shard_map/put/pallas_call | solution.py:564

commit v6 on v5

--- a/solution.py
+++ b/solution.py
@@ -79,6 +79,11 @@
         return dict(device_id={"tp": dev}, device_id_type=MESH)
 
     def loop(n, body):
+        if n == 3:
+            for i in range(n):
+                body(i)
+            return
+
         def step(i, _):
             body(i)
             return 0

time: 404 us -> 402 us (level)
  no operation moved by 1% of the time
where the time goes in v6:
time: 402 us
  Pallas kernels  402 us (100%)
    pallas_call x1, Pallas kernels, block(): pl.pallas_call(kernel, name='mlp', out_shape=[jax.ShapeDtypeStruct((rows,...  377 us
    pallas_call x1, Pallas kernels, block(): pl.pallas_call(put, name='put', out_shape=jax.ShapeDtypeStruct((rows, dep...  24.8 us

profile of v6, /device:TPU:0, one launch (start us, length us, event | category | flops | bytes accessed | tf_op | source)
XLA Modules:
  0.0 402.0 jit_solution(18015875607159789037)
XLA Ops:
  0.0 377.2 %mlp.1 = (bf16[2048,12288]{1,0:T(8,128)(2,1)}, bf16[3,6144,512]{2,1,0:T(8,128)(2,1)S(1)}, bf16[2,352,6144]{2,1,0:T(8,128)(2,1)S(1)}) custom-call(bf16[2048,12288]{1,0:T(8,128)(2,1)} %x_hbm.1, bf16[12288,1792]{1,0:T(8,128)(2,1)} %wg_hbm.1, bf16[12288,1792]{1,0:T(8,128)(2,1)} %wu_hbm.1, bf16[1792,12288]{1,0:T(8,128)(2,1)} %wd_hbm.1), custom_call_target="tpu_custom_call" | custom-call | tf_op jit(solution)/shard_map/mlp/pallas_call | solution.py:536
  377.2 24.8 %put.1 = bf16[2048,12288]{1,0:T(8,128)(2,1)} custom-call(bf16[2048,12288]{1,0:T(8,128)(2,1)} %get-tuple-element.8.y_hbm, bf16[3,6144,512]{2,1,0:T(8,128)(2,1)S(1)} %get-tuple-element.9.wbuf, bf16[2,352,6144]{2,1,0:T(8,128)(2,1)S(1)} %get-tuple-element.10.xv), custom_call_target="tpu_custom_call" | custom-call | tf_op jit(solution)/shard_map/put/pallas_call | solution.py:569

commit v7 on v6

--- a/solution.py
+++ b/solution.py
@@ -490,20 +490,22 @@
 
     def chunk(c):
         def tile(n):
-            @pl.when((c == nc) & (n == 1))
-            def _():
-                loop(nc - 2, lambda i: big.a0_wait(i))
-                keep(lambda cp: cp.start())
-
             for i in range(PACKETS):
                 either(c, lambda a: a.gate_up(c, n, i))
                 if i == 0:
                     pl.when((c == 0) & (n >= 3) & (n < 6))(lambda: d_copy(n - 3).start())
 
-                for slot, act, lag in SLOTS:
-                    if slot % PACKETS == i:
-                        pl.when(n == slot // PACKETS)(
-                            lambda act=act, lag=lag: either(c - lag, lambda a: getattr(a, act)(c - lag)))
+                for slot in sorted({slot for slot, _, _ in SLOTS if slot % PACKETS == i}):
+                    @pl.when(n == slot // PACKETS)
+                    def _(slot=slot):
+                        for at, act, lag in SLOTS:
+                            if at == slot:
+                                either(c - lag, lambda a, act=act, lag=lag: getattr(a, act)(c - lag))
+                        if slot == 1:
+                            @pl.when(c == nc)
+                            def _():
+                                loop(nc - 2, lambda i: big.a0_wait(i))
+                                keep(lambda cp: cp.start())
 
         loop(nt, tile)
         either(c, lambda a: a.early(c))

time: 402 us -> 402 us (level)
  no operation moved by 1% of the time
where the time goes in v7:
time: 402 us
  Pallas kernels  402 us (100%)
    pallas_call x1, Pallas kernels, block(): pl.pallas_call(kernel, name='mlp', out_shape=[jax.ShapeDtypeStruct((rows,...  377 us
    pallas_call x1, Pallas kernels, block(): pl.pallas_call(put, name='put', out_shape=jax.ShapeDtypeStruct((rows, dep...  24.8 us

profile of v7, /device:TPU:0, one launch (start us, length us, event | category | flops | bytes accessed | tf_op | source)
XLA Modules:
  0.0 401.9 jit_solution(8911558884477569881)
XLA Ops:
  0.0 377.1 %mlp.1 = (bf16[2048,12288]{1,0:T(8,128)(2,1)}, bf16[3,6144,512]{2,1,0:T(8,128)(2,1)S(1)}, bf16[2,352,6144]{2,1,0:T(8,128)(2,1)S(1)}) custom-call(bf16[2048,12288]{1,0:T(8,128)(2,1)} %x_hbm.1, bf16[12288,1792]{1,0:T(8,128)(2,1)} %wg_hbm.1, bf16[12288,1792]{1,0:T(8,128)(2,1)} %wu_hbm.1, bf16[1792,12288]{1,0:T(8,128)(2,1)} %wd_hbm.1), custom_call_target="tpu_custom_call" | custom-call | tf_op jit(solution)/shard_map/mlp/pallas_call | solution.py:538
  377.1 24.8 %put.1 = bf16[2048,12288]{1,0:T(8,128)(2,1)} custom-call(bf16[2048,12288]{1,0:T(8,128)(2,1)} %get-tuple-element.8.y_hbm, bf16[3,6144,512]{2,1,0:T(8,128)(2,1)S(1)} %get-tuple-element.9.wbuf, bf16[2,352,6144]{2,1,0:T(8,128)(2,1)S(1)} %get-tuple-element.10.xv), custom_call_target="tpu_custom_call" | custom-call | tf_op jit(solution)/shard_map/put/pallas_call | solution.py:571
